TPU v7x, 128 devices: a whole 4x4x4 slice. The times are simulated.
128 devices in a mesh: ic: 4 (over z_lo, core), member: 2 (over z_hi), lat: 16 (over x, y).
Axes of the slice: x: 4, y: 4, z: 4 (z_hi: 2, z_lo: 2; z = z_hi * 2 + z_lo), core: 2. Of those that a mesh axis runs over, the one named last changes fastest.
Arguments:
- state: bfloat16 [8, 640, 32, 2560], P(('ic', 'member'), 'lat'), parts along dimension 0, may hold values from -6 to 6
- target: bfloat16 [2560, 32, 2560], P(('ic', 'lat')), parts along dimension 0, may hold values from -6 to 6
- noise: float32 [8, 640, 32, 320], P(('ic', 'member'), 'lat'), parts along dimension 0, may hold values from -4 to 4
- gain: float32 [640, 320], P('lat'), may hold values from 0.2 to 1
- vertical_mix: float32 [32, 32], replicated, may hold values from -1 to 1
Outputs:
- new_state: bfloat16 [8, 640, 32, 2560], P(('ic', 'member'), 'lat'), parts along dimension 0
- crps: float32 [8, 640, 2560], P(('ic', 'member'), 'lat'), parts along dimension 0
There are 4 independent parts, one for each index of `ic`. A program takes and returns all parts, laid end to end along the dimension named above; an argument that names none is the same for every part. Nothing has to cross between parts.
All inputs are finite; a program needn't handle non-finite values.
Results may differ from a plain program's by a relative error of at most 0.0042.
Values may be sent and summed in bfloat16 or wider, within the bound.
No kernel may reach another device: no remote copies, remote signals or barrier semaphores. Data moves between devices by JAX's collectives and lax.ppermute only.
A program may use at most 128 MiB of HBM per device.

v0:
```python
import math

import jax
import jax.numpy as jnp
from jax import lax
from jax.sharding import PartitionSpec as P

NLON = 2560
NLAT = 640
MW = 320


def split_up(x, dim, count):
    dims = x.shape
    blocks = x.reshape(*dims[:dim], count, dims[dim] // count, *dims[dim + 1 :])
    return jnp.moveaxis(blocks, dim, 0)


def cut_rows(length, count):
    step = length // count
    if step >= 8:
        step -= step % 8
    return [step * k for k in range(1, count)]


def laid_out(blocks, dim):
    blocks = jnp.moveaxis(blocks, 0, dim)
    dims = blocks.shape
    return blocks.reshape(*dims[:dim], dims[dim] * dims[dim + 1], *dims[dim + 2 :])


def several_exchanges(x, axis, pieces, split_dim, concat_dim):
    blocks = split_up(x, split_dim, lax.axis_size(axis))
    split_at = max(range(1, max(2, blocks.ndim - 1)), key=lambda d: blocks.shape[d])
    done = []
    for section in jnp.split(blocks, cut_rows(blocks.shape[split_at], pieces), axis=split_at):
        if section.size:
            done.append(lax.all_to_all(section, axis, split_axis=0, concat_axis=0, tiled=True))
    return laid_out(jnp.concatenate(done, axis=split_at), concat_dim)


def column_info():
    column = jnp.arange(2 * MW, dtype=jnp.int32)
    part = column // MW
    rest = column % MW
    half = MW // 2
    wave = jnp.where(rest < half, 2 * rest + 2 * part, 2 * (rest - half) + 1)
    return (part, wave)


def lon_table():
    part, wave = column_info()
    place = jnp.arange(NLON, dtype=jnp.int32)
    phase = place[:, None] * wave[None, :] % NLON
    angle = phase.astype(jnp.float32) * jnp.float32(2.0 * math.pi / NLON)
    return jnp.where(part[None, :] == 0, jnp.cos(angle), jnp.sin(angle)).astype(jnp.bfloat16)


def lat_basis(is_odd):
    theta = (jnp.arange(NLAT, dtype=jnp.float32) + 0.5) * jnp.float32(math.pi / NLAT)
    modes = jnp.arange(NLAT // 2, dtype=jnp.float32)
    even = jnp.cos(modes[:, None] * theta[None, :])
    odd_basis = jnp.sin((modes[:, None] + 1.0) * theta[None, :])
    return jnp.where(is_odd, odd_basis, even)


def member_score(own, other, truth):
    own = own.astype(jnp.float32)
    other = other.astype(jnp.float32)
    truth = truth.astype(jnp.float32)
    skill = jnp.mean(jnp.abs(own - truth), axis=1)
    spread = jnp.mean(jnp.abs(own - other), axis=1)
    return skill - 0.5 * spread


def body(state, target, noise, gain, vertical_mix):
    field = state[0]
    rows = field.shape[0]
    levels = field.shape[1]
    modes = NLAT // 2
    highest = lax.Precision.HIGHEST
    table = lon_table()
    zonal = jnp.dot(field.reshape(rows * levels, NLON), table, preferred_element_type=jnp.float32)
    zonal = (zonal * jnp.float32(1.0 / math.sqrt(NLON))).reshape(rows, levels, 2 * MW)
    gathered = lax.all_to_all(zonal, "lat", split_axis=2, concat_axis=0, tiled=True)
    width = gathered.shape[2]
    first_col = lax.axis_index("lat") * width
    basis = lat_basis(first_col % MW >= MW // 2)
    spectral = jnp.dot(basis, gathered.reshape(NLAT, levels * width), precision=highest)
    spectral = spectral.reshape(modes, levels, width) * jnp.float32(math.sqrt(2.0 / NLAT))
    forced = gain.T[:, None, :] * spectral + jnp.transpose(noise[0], (2, 1, 0))
    back = jnp.dot(basis.T, forced.reshape(modes, levels * width), precision=highest)
    back = (back.reshape(NLAT, levels, width) * jnp.float32(math.sqrt(2.0 / modes))).astype(
        jnp.bfloat16
    )
    returned = lax.all_to_all(back, "lat", split_axis=0, concat_axis=2, tiled=True)
    tendency = lax.dot_general(
        returned.reshape(rows * levels, 2 * MW),
        table,
        (((1,), (1,)), ((), ())),
        preferred_element_type=jnp.float32,
    )
    tendency = (tendency * jnp.float32(1.0 / math.sqrt(MW))).reshape(rows, levels, NLON)
    mixed = jnp.einsum("ab,jbi->jai", vertical_mix, tendency, precision=highest)
    updated = (field.astype(jnp.float32) + mixed).astype(jnp.bfloat16)
    half = NLON // 2
    paired = several_exchanges(updated[None], "member", 2, 3, 0)
    truth = lax.dynamic_slice_in_dim(target, lax.axis_index("member") * half, half, 2)
    both_scores = jnp.stack(
        [member_score(paired[0], paired[1], truth), member_score(paired[1], paired[0], truth)],
        axis=0,
    )
    crps = lax.all_to_all(both_scores, "member", split_axis=0, concat_axis=2, tiled=True)
    return (updated[None], crps)


def solution(mesh):
    placed = (
        P(("ic", "member"), "lat", None, None),
        P(("ic", "lat"), None, None),
        P(("ic", "member"), "lat", None, None),
        P("lat", None),
        P(),
    )
    return jax.shard_map(
        body,
        mesh=mesh,
        in_specs=placed,
        out_specs=(P(("ic", "member"), "lat", None, None), P(("ic", "member"), "lat", None)),
        check_vma=False,
    )
```

profile of v0, /device:TPU:0, one launch (start us, length us, event | category | flops | bytes accessed | tf_op | source)
XLA Modules:
  0.0 441.7 jit_solution(3785147405291336206)
XLA Ops:
  0.7 36.2 %fusion.14 = f32[1280,640]{0,1:T(8,128)} fusion(bf16[1280,2560]{1,0:T(8,128)(2,1)} %bitcast.104, s32[640]{0:T(1024)S(1)} %fusion.42, pred[640]{0:T(1024)(128)(4,1)S(1)} %broadcast_compare_fusion), kind=kOutput, calls=%fused_computation.26 | convolution fusion | flops 4213145600 | bytes 9833600 | tf_op jit(solution)/shard_map/dot_general | solution.py:83
  40.4 9.2 %copy.33 = f32[40,32,640]{0,1,2:T(8,128)} copy(f32[40,32,640]{2,1,0:T(8,128)S(1)} %bitcast.103) | data formatting | bytes 6553600 | tf_op jit(solution)/shard_map/reshape | solution.py:84
  49.6 15.5 %reshape.129 = f32[16,1,51200]{2,1,0:T(1,128)} reshape(f32[640,32,40]{2,1,0:T(8,128)} %bitcast.95) | data formatting | bytes 6553600
  65.0 7.5 %all-to-all-start = ((f32[16,1,51200]{2,1,0:T(1,128)}), f32[16,1,51200]{2,1,0:T(1,128)S(1)}, u32[]{:S(2)}, u32[]{:S(2)}) async-start(f32[16,1,51200]{2,1,0:T(1,128)} %reshape.129), calls=%async_computation | async-start | bytes 6553600 | tf_op jit(solution)/shard_map/all_to_all | solution.py:85
  72.6 43.8 %all-to-all-done = f32[16,1,51200]{2,1,0:T(1,128)S(1)} async-done(((f32[16,1,51200]{2,1,0:T(1,128)}), f32[16,1,51200]{2,1,0:T(1,128)S(1)}, u32[]{:S(2)}, u32[]{:S(2)}) %all-to-all-start) | async-done | bytes 3276832 | tf_op jit(solution)/shard_map/all_to_all | solution.py:85
  116.9 11.1 %reduce = f32[16,51200]{1,0:T(8,128)} reduce(f32[16,1,51200]{2,1,0:T(1,128)S(1)} %all-to-all-done, f32[]{:T(128)} %broadcast.164), dimensions={1}, to_apply=%all_to_all.41.reduce_sub_computation | reduce | bytes 6553604 | tf_op jit(solution)/shard_map/all_to_all | solution.py:85
  128.1 16.3 %reshape.130 = f32[640,32,40]{2,1,0:T(8,128)} reshape(f32[16,51200]{1,0:T(8,128)} %reduce) | data formatting | bytes 6553600
  144.4 13.9 %copy.34 = f32[16,40,32,40]{1,0,3,2:T(8,128)} copy(f32[16,40,32,40]{1,2,3,0:T(8,128)} %bitcast.94) | data formatting | bytes 6553600 | tf_op jit(solution)/shard_map/all_to_all | solution.py:85
  158.2 8.6 %reshape.120 = f32[640,1280]{0,1:T(8,128)S(1)} reshape(f32[16,40,32,40]{1,0,3,2:T(8,128)} %copy.34) | data formatting | bytes 6553600 | tf_op jit(solution)/shard_map/reshape | solution.py:89
  166.8 11.4 %fusion.23 = f32[320,32,40]{0,2,1:T(8,128)S(1)} fusion(f32[32,40,640]{2,1,0:T(8,128)S(1)} %bitcast.101, f32[640]{0:T(1024)S(1)} %add_multiply_fusion, f32[320]{0:T(512)S(1)} %iota_add_fusion, pred[]{:T(512)S(6)} %ge.3), kind=kOutput, calls=%fused_computation.37 | convolution fusion | flops 3146342400 | bytes 4919041 | tf_op jit(solution)/shard_map/dot_general | solution.py:89
  178.3 14.4 %multiply_convert_fusion = bf16[640,32,40]{0,2,1:T(8,128)(2,1)S(1)} fusion(f32[1,40,32,320]{3,2,1,0:T(8,128)} %param.7, f32[320,32,40]{0,2,1:T(8,128)S(1)} %fusion.23, f32[320,40]{0,1:T(8,128)S(1)} %multiply_bitcast_fusion, f32[640]{0:T(1024)S(1)} %add_multiply_fusion, f32[320]{0:T(512)S(1)} %iota_add_fusion, pred[]{:T(512)S(6)} %ge.3), kind=kOutput, calls=%fused_computation.29 | convolution fusion | flops 3148800000 | bytes 4970241 | tf_op jit(solution)/shard_map/dot_general | solution.py:92
  192.7 7.9 %copy.36 = bf16[640,32,40]{2,1,0:T(8,128)(2,1)} copy(bf16[640,32,40]{0,2,1:T(8,128)(2,1)S(1)} %multiply_convert_fusion) | data formatting | bytes 3276800 | tf_op jit(solution)/shard_map/convert_element_type | solution.py:93
  200.6 9.3 %reshape.131 = bf16[16,2,25600]{2,1,0:T(2,128)(2,1)S(1)} reshape(bf16[640,32,40]{2,1,0:T(8,128)(2,1)} %copy.36) | data formatting | bytes 3276800
  209.9 30.5 %all_to_all.58 = bf16[16,2,25600]{2,1,0:T(2,128)(2,1)S(1)} all-to-all(bf16[16,2,25600]{2,1,0:T(2,128)(2,1)S(1)} %reshape.131), channel_id=1, replica_groups=mesh['ic'=4,'member'=2,'lat'=16] {'lat'}, dimensions={0} | all-to-all | bytes 3276800 | tf_op jit(solution)/shard_map/all_to_all | solution.py:96
  240.4 8.9 %reshape.132 = bf16[640,32,40]{2,1,0:T(8,128)(2,1)} reshape(bf16[16,2,25600]{2,1,0:T(2,128)(2,1)S(1)} %all_to_all.58) | data formatting | bytes 3276800
  249.3 10.9 %copy.50 = bf16[16,40,32,40]{3,0,2,1:T(8,128)(2,1)} copy(bf16[16,40,32,40]{3,2,1,0:T(8,128)(2,1)} %bitcast.99) | data formatting | bytes 3276800 | tf_op jit(solution)/shard_map/all_to_all | solution.py:96
  260.2 7.4 %reshape.122 = bf16[1280,640]{1,0:T(8,128)(2,1)S(1)} reshape(bf16[40,32,16,40]{3,2,1,0:T(8,128)(2,1)} %bitcast.100) | data formatting | bytes 3276800 | tf_op jit(solution)/shard_map/reshape | solution.py:98
  267.6 29.8 %convolution_multiply_fusion = f32[1280,2560]{1,0:T(8,128)S(1)} fusion(bf16[1280,640]{1,0:T(8,128)(2,1)S(1)} %reshape.122, s32[640]{0:T(1024)S(1)} %fusion.42, pred[640]{0:T(1024)(128)(4,1)S(1)} %broadcast_compare_fusion), kind=kOutput, calls=%fused_computation | convolution fusion | flops 4215603200 | bytes 14748800 | tf_op jit(solution)/shard_map/dot_general | solution.py:97
  297.5 15.3 %fusion = bf16[40,32,2560]{2,1,0:T(8,128)(2,1)} fusion(f32[40,32,2560]{2,1,0:T(8,128)S(1)} %bitcast.102, bf16[1,40,32,2560]{3,2,1,0:T(8,128)(2,1)} %param.5, f32[32,32]{1,0:T(8,128)S(1)} %copy-done), kind=kOutput, calls=%fused_computation.2 | convolution fusion | flops 1268121600 | bytes 26218496 | tf_op jit(solution)/shard_map/ab,jbi->jai/dot_general | solution.py:104
  312.7 14.1 %reshape_broadcast_in_dim.3 = bf16[1,40,32,2,1280]{4,3,2,1,0:T(2,128)(2,1)} reshape(bf16[40,32,2560]{2,1,0:T(8,128)(2,1)} %fusion) | data formatting | bytes 13107200 | tf_op jit(solution)/shard_map/reshape;broadcast_in_dim | solution.py:15
  345.0 25.1 %all-to-all-done.2 = bf16[2,1,16,32,1280]{4,3,2,1,0:T(8,128)(2,1)S(1)} async-done(((bf16[2,1,16,32,1280]{4,3,2,1,0:T(8,128)(2,1)}), bf16[2,1,16,32,1280]{4,3,2,1,0:T(8,128)(2,1)S(1)}, u32[]{:S(2)}, u32[]{:S(2)}) %all-to-all-start.2) | async-done | bytes 2621472 | tf_op jit(solution)/shard_map/all_to_all | solution.py:38
  377.3 41.1 %all-to-all-done.3 = bf16[2,1,24,32,1280]{4,3,2,1,0:T(8,128)(2,1)} async-done(((bf16[2,1,24,32,1280]{4,3,2,1,0:T(8,128)(2,1)}), bf16[2,1,24,32,1280]{4,3,2,1,0:T(8,128)(2,1)}, u32[]{:S(2)}, u32[]{:S(2)}) %all-to-all-start.3) | async-done | bytes 3932192 | tf_op jit(solution)/shard_map/all_to_all | solution.py:38
  422.6 8.1 %fusion.4 = (f32[40,1280]{1,0:T(8,128)S(1)}, f32[40,1280]{1,0:T(8,128)S(1)}, f32[40,1280]{1,0:T(8,128)S(1)}, f32[40,1280]{1,0:T(8,128)S(1)}) fusion(bf16[40,32,2560]{2,1,0:T(8,128)(2,1)} %param.6, s32[]{:T(128)S(6)} %select_n.75, bf16[2,1,40,32,1280]{4,3,2,1,0:T(8,128)(2,1)} %constant_dynamic-update-slice_fusion), kind=kLoop, calls=%fused_computation.11 | loop fusion | flops 24371200 | bytes 10649604 | tf_op jit(solution)/shard_map/reduce_sum | solution.py:71
  430.8 9.8 %all_to_all.59 = f32[2,40,1280]{2,1,0:T(8,128)S(1)} all-to-all(f32[2,40,1280]{2,1,0:T(8,128)S(1)} %pad_maximum_fusion), channel_id=1, replica_groups=mesh['ic'=4,'member'=2,'lat'=16] {'member'}, dimensions={0} | all-to-all | bytes 819200 | tf_op jit(solution)/shard_map/all_to_all | solution.py:113
  (23 shorter events, 34.4 us)
Async XLA Ops:
  0.6 296.8 %copy-start = (f32[32,32]{1,0:T(8,128)S(1)}, f32[32,32]{1,0:T(8,128)}, u32[]{:S(2)}) copy-start(f32[32,32]{1,0:T(8,128)} %param.9) | copy-start | bytes 12292
  65.0 7.5 %copy-start.2 = (f32[40,320]{1,0:T(8,128)S(1)}, f32[40,320]{1,0:T(8,128)}, u32[]{:S(2)}) copy-start(f32[40,320]{1,0:T(8,128)} %param.8) | copy-start | bytes 153604
  65.0 51.4 %all-to-all-start = ((f32[16,1,51200]{2,1,0:T(1,128)}), f32[16,1,51200]{2,1,0:T(1,128)S(1)}, u32[]{:S(2)}, u32[]{:S(2)}) async-start(f32[16,1,51200]{2,1,0:T(1,128)} %reshape.129), calls=%async_computation | async-start | bytes 6553600 | tf_op jit(solution)/shard_map/all_to_all | solution.py:85
  331.1 2.7 copy-start.1
  335.5 34.7 %all-to-all-start.2 = ((bf16[2,1,16,32,1280]{4,3,2,1,0:T(8,128)(2,1)}), bf16[2,1,16,32,1280]{4,3,2,1,0:T(8,128)(2,1)S(1)}, u32[]{:S(2)}, u32[]{:S(2)}) async-start(bf16[2,1,16,32,1280]{4,3,2,1,0:T(8,128)(2,1)} %split.8), calls=%async_computation.2 | async-start | bytes 5242880 | tf_op jit(solution)/shard_map/all_to_all | solution.py:38
  370.2 48.2 %all-to-all-start.3 = ((bf16[2,1,24,32,1280]{4,3,2,1,0:T(8,128)(2,1)}), bf16[2,1,24,32,1280]{4,3,2,1,0:T(8,128)(2,1)}, u32[]{:S(2)}, u32[]{:S(2)}) async-start(bf16[2,1,24,32,1280]{4,3,2,1,0:T(8,128)(2,1)} %split.9), calls=%async_computation.3 | async-start | bytes 7864320 | tf_op jit(solution)/shard_map/all_to_all | solution.py:38
where the time goes:
time: 448 us; the launch traced here: 442 us
  local copies, waits for them, and re-layouts  146 us (33%)
  waiting for transfers between devices  110 us (25%)
  matrix products  107 us (24%)
  blocking collectives  40.3 us (9%)
  other arithmetic  19.4 us (4%)
  starting transfers between devices  18.1 us (4%)
    all_to_all x2, waiting for transfers between devices, several_exchanges(): lax.all_to_all(section, axis, split_axis=0, concat_axis=0, tiled=True)  66.2 us
    unnamed x11, local copies, waits for them, and re-layouts  54.4 us
    all_to_all x1, waiting for transfers between devices, body(): lax.all_to_all(zonal, 'lat', split_axis=2, concat_axis=0, tiled=True)  43.8 us
    dot_general x1, matrix products, body(): jnp.dot(field.reshape(rows * levels, NLON), table, preferred_element_type...  36.2 us
    all_to_all x1, blocking collectives, body(): lax.all_to_all(back, 'lat', split_axis=0, concat_axis=2, tiled=True)  30.5 us
    dot_general x1, matrix products, body(): lax.dot_general(returned.reshape(rows * levels, 2 * MW), table, (((1,), (...  29.8 us
    another operation x2, local copies, waits for them, and re-layouts, split_up(): blocks = x.reshape(*dims[:dim], count, dims[dim] // count, *dims[dim + 1:])  18.3 us
    dot_general x1, matrix products, body(): mixed = jnp.einsum('ab,jbi->jai', vertical_mix, tendency, precision=highest)  15.3 us
  transfers between devices with their start and end apart: 3, of which 3 were waited for; matrix products, arithmetic and copies ran while one was open for 1% of the time, Pallas kernels for 0%

commit v1 on v0

v1 whole, which is shorter than its diff:
```python
import functools
import math

import jax
import jax.numpy as jnp
import ml_dtypes
import numpy as np
from jax import lax
from jax.experimental import pallas as pl
from jax.experimental.pallas import tpu as pltpu
from jax.sharding import PartitionSpec as P

NLON = 2560
NLAT = 640
MW = 320
LEVELS = 32
NK = 320
NCOL = 2 * MW
LAT = 16
ROWS = NLAT // LAT
OWN = NCOL // LAT
HALF = LEVELS // 2
TILES = OWN // 8
GROUPS = ROWS // 8
BF16 = jnp.bfloat16
F32 = jnp.float32
HIGHEST = lax.Precision.HIGHEST


def column_order():
    n = np.arange(NCOL)
    return 40 * ((n % 128) // 8) + 8 * (n // 128) + n % 8


def lon_table():
    column = column_order()
    part = column // MW
    rest = column % MW
    half = MW // 2
    wave = np.where(rest < half, 2 * rest + 2 * part, 2 * (rest - half) + 1)
    phase = np.arange(NLON)[:, None] * wave[None, :] % NLON
    angle = 2.0 * math.pi / NLON * phase
    table = np.where(part[None, :] == 0, np.cos(angle), np.sin(angle))
    return table.astype(np.float32).astype(ml_dtypes.bfloat16)


def lat_bases():
    theta = (np.arange(NLAT) + 0.5) * (math.pi / NLAT)
    modes = np.arange(NK)
    even = np.cos(modes[:, None] * theta[None, :])
    odd = np.sin((modes[:, None] + 1.0) * theta[None, :])
    both = np.stack([even, odd]).astype(np.float32)
    high = both.astype(ml_dtypes.bfloat16)
    low = (both - high.astype(np.float32)).astype(ml_dtypes.bfloat16)
    return high, low


def swap_groups(v):
    v = list(v)
    lane = lax.broadcasted_iota(jnp.int32, v[0].shape, 1)
    for bit in range(4):
        shift = 8 << bit
        upper = (lane & shift) != 0
        for a in range(16):
            if a & (1 << bit):
                continue
            first, second = v[a], v[a | (1 << bit)]
            v[a] = jnp.where(upper, pltpu.roll(second, shift, 1), first)
            v[a | (1 << bit)] = jnp.where(upper, second, pltpu.roll(first, 128 - shift, 1))
    return v


def forward_kernel(x_ref, table_ref, out_ref, held):
    zonal = jnp.dot(x_ref[...], table_ref[...], preferred_element_type=F32)
    for t in range(TILES):
        for j in range(8):
            held[t, 40 * j : 40 * j + 32, :] = zonal[32 * j : 32 * j + 32, 128 * t : 128 * (t + 1)]
    for t in range(TILES):
        for h in range(2):
            v = [held[t, pl.ds(HALF * h + a, 8, stride=40), :] for a in range(16)]
            lanes = slice(128 * (2 * t + h), 128 * (2 * t + h + 1))
            for q, w in enumerate(swap_groups(v)):
                out_ref[q, :, lanes] = w.astype(BF16)


def forward(field, table):
    rows = field.shape[0]
    return pl.pallas_call(
        forward_kernel,
        grid=(GROUPS,),
        in_specs=[
            pl.BlockSpec((rows // GROUPS, NLON), lambda i: (i, 0)),
            pl.BlockSpec((NLON, NCOL), lambda i: (0, 0)),
        ],
        out_specs=pl.BlockSpec((LAT, 8, OWN * LEVELS), lambda i: (0, i, 0)),
        out_shape=jax.ShapeDtypeStruct((LAT, ROWS, OWN * LEVELS), BF16),
        scratch_shapes=[pltpu.VMEM((TILES, 8 * 40, 128), F32)],
        cost_estimate=pl.CostEstimate(
            flops=2 * rows * NLON * NCOL, bytes_accessed=12_000_000, transcendentals=0
        ),
        name="forward_lon",
    )(field, table)


def prepare_kernel(noise_ref, mix_ref, gain_ref, pick_ref, mixed_ref, wide_ref):
    contract = (((0,), (0,)), ((), ()))
    mixed_ref[...] = lax.dot_general(
        noise_ref[...], mix_ref[...], contract, precision=HIGHEST, preferred_element_type=F32
    )
    wide_ref[...] = lax.dot_general(
        gain_ref[...], pick_ref[...], contract, precision=HIGHEST, preferred_element_type=F32
    )


def prepare(noise, mix, gain, pick):
    wide = OWN * LEVELS
    return pl.pallas_call(
        prepare_kernel,
        grid=(TILES,),
        in_specs=[
            pl.BlockSpec((256, NK), lambda t: (t, 0)),
            pl.BlockSpec((256, 256), lambda t: (0, 0)),
            pl.BlockSpec((OWN, NK), lambda t: (0, 0)),
            pl.BlockSpec((OWN, 256), lambda t: (0, t)),
        ],
        out_specs=[
            pl.BlockSpec((NK, 256), lambda t: (0, t)),
            pl.BlockSpec((NK, 256), lambda t: (0, t)),
        ],
        out_shape=[jax.ShapeDtypeStruct((NK, wide), F32)] * 2,
        cost_estimate=pl.CostEstimate(
            flops=12 * 256 * NK * wide, bytes_accessed=6_000_000, transcendentals=0
        ),
        name="prepare_noise",
    )(noise, mix, gain, pick)


def halves(x):
    high = x.astype(BF16)
    return high, (x - high.astype(F32)).astype(BF16)


def mm(a, b):
    return jnp.dot(a, b, preferred_element_type=F32)


def spectral_kernel(odd, g_ref, bh_ref, bl_ref, th_ref, tl_ref, mh_ref, ml_ref, noise_ref, gain_ref, send_ref, keep_ref):
    g = g_ref[...]
    forced = (mm(bh_ref[0], g) + mm(bl_ref[0], g)) * gain_ref[...]
    high, low = halves(forced)
    mixed = mm(high, mh_ref[...]) + mm(low, mh_ref[...]) + mm(high, ml_ref[...]) + noise_ref[...]
    high, low = halves(mixed)
    back = mm(th_ref[0], high) + mm(th_ref[0], low) + mm(tl_ref[0], high)
    back = (back * F32(math.sqrt(2.0) / NK)).astype(BF16)
    send_ref[...] = back[:, :128]
    keep_ref[...] = back[:, 128:]


def spectral(odd, gathered, bases, mixes, noise, gain):
    def whole(shape):
        return pl.BlockSpec((1,) + shape, lambda t, odd: (odd[0], 0, 0))

    mix_spec = pl.BlockSpec((256, 256), lambda t, odd: (0, 0))
    tile_spec = pl.BlockSpec((NK, 256), lambda t, odd: (0, t))
    half_spec = pl.BlockSpec((NLAT, 128), lambda t, odd: (0, t))
    return pl.pallas_call(
        spectral_kernel,
        grid_spec=pltpu.PrefetchScalarGridSpec(
            num_scalar_prefetch=1,
            grid=(TILES,),
            in_specs=[
                pl.BlockSpec((NLAT, 256), lambda t, odd: (0, t)),
                whole((NK, NLAT)),
                whole((NK, NLAT)),
                whole((NLAT, NK)),
                whole((NLAT, NK)),
                mix_spec,
                mix_spec,
                tile_spec,
                tile_spec,
            ],
            out_specs=[half_spec, half_spec],
        ),
        out_shape=[jax.ShapeDtypeStruct((NLAT, TILES * 128), BF16)] * 2,
        cost_estimate=pl.CostEstimate(
            flops=4_000_000_000, bytes_accessed=10_000_000, transcendentals=0
        ),
        name="spectral_step",
    )(odd, gathered, *bases, *mixes, noise, gain)


def rows_of(coef_ref, held):
    for t in range(TILES):
        v = [coef_ref[q, :, 128 * t : 128 * (t + 1)].astype(F32) for q in range(LAT)]
        for a, w in enumerate(swap_groups(v)):
            held[t, pl.ds(a, 8, stride=24), :] = w
    tiles = [
        jnp.concatenate([held[t, 24 * j : 24 * j + 16, :] for j in range(8)], axis=0)
        for t in range(TILES)
    ]
    return jnp.concatenate(tiles, axis=1).astype(BF16)


CHUNK = 640


def own_kernel(where, coef_ref, state_ref, target_ref, table_ref, *rest):
    new_ref, skill_ref, held = rest[-3:]
    rows = rows_of(coef_ref, held)
    for n in range(0, NLON, CHUNK):
        cut = slice(n, n + CHUNK)
        tendency = mm(rows, table_ref[:, cut]).reshape(8, HALF, CHUNK)
        new = (state_ref[:, :, cut].astype(F32) + tendency).astype(BF16)
        new_ref[:, :, cut] = new
        skill_ref[:, cut] = jnp.sum(
            jnp.abs(new.astype(F32) - target_ref[:, :, cut].astype(F32)), axis=1
        )


def own_step(where, coef, state, target, table, into=None):
    level_spec = pl.BlockSpec((8, HALF, NLON), lambda i, where: (i, where[0], 0))
    extra = [] if into is None else [into]
    return pl.pallas_call(
        own_kernel,
        grid_spec=pltpu.PrefetchScalarGridSpec(
            num_scalar_prefetch=1,
            grid=(GROUPS,),
            in_specs=[
                pl.BlockSpec((LAT, 8, TILES * 128), lambda i, where: (0, i, 0)),
                level_spec,
                level_spec,
                pl.BlockSpec((NCOL, NLON), lambda i, where: (0, 0)),
            ]
            + [pl.BlockSpec(memory_space=pl.ANY) for _ in extra],
            out_specs=[level_spec, pl.BlockSpec((8, NLON), lambda i, where: (i, 0))],
            scratch_shapes=[pltpu.VMEM((TILES, 8 * 24, 128), F32)],
        ),
        out_shape=[
            jax.ShapeDtypeStruct((ROWS, LEVELS, NLON), BF16),
            jax.ShapeDtypeStruct((ROWS, NLON), F32),
        ],
        input_output_aliases={} if into is None else {5: 0},
        cost_estimate=pl.CostEstimate(
            flops=2 * ROWS * HALF * NCOL * NLON, bytes_accessed=14_000_000, transcendentals=0
        ),
        name="own_step",
    )(where, coef, state, target, table, *extra)


def other_kernel(where, coef_ref, state_ref, own_ref, table_ref, spread_ref, held):
    rows = rows_of(coef_ref, held)
    for n in range(0, NLON, CHUNK):
        cut = slice(n, n + CHUNK)
        tendency = mm(rows, table_ref[:, cut]).reshape(8, HALF, CHUNK)
        new = (state_ref[:, :, cut].astype(F32) + tendency).astype(BF16)
        spread_ref[:, cut] = jnp.sum(
            jnp.abs(new.astype(F32) - own_ref[:, :, cut].astype(F32)), axis=1
        )


def other_step(where, coef, state, own, table):
    return pl.pallas_call(
        other_kernel,
        grid_spec=pltpu.PrefetchScalarGridSpec(
            num_scalar_prefetch=1,
            grid=(GROUPS,),
            in_specs=[
                pl.BlockSpec((LAT, 8, TILES * 128), lambda i, where: (0, i, 0)),
                pl.BlockSpec((8, HALF, NLON), lambda i, where: (i, 0, 0)),
                pl.BlockSpec((8, HALF, NLON), lambda i, where: (i, where[0], 0)),
                pl.BlockSpec((NCOL, NLON), lambda i, where: (0, 0)),
            ],
            out_specs=pl.BlockSpec((8, NLON), lambda i, where: (i, 0)),
            scratch_shapes=[pltpu.VMEM((TILES, 8 * 24, 128), F32)],
        ),
        out_shape=jax.ShapeDtypeStruct((ROWS, NLON), F32),
        cost_estimate=pl.CostEstimate(
            flops=2 * ROWS * HALF * NCOL * NLON, bytes_accessed=12_000_000, transcendentals=0
        ),
        name="other_step",
    )(where, coef, state, own, table)


def to_partner(x):
    return lax.ppermute(x, "member", [(0, 1), (1, 0)])


def over_lat(x):
    return lax.all_to_all(x, "lat", split_axis=0, concat_axis=0, tiled=True)


def body(state, target, noise, gain, vertical_mix):
    member = lax.axis_index("member")
    lat = lax.axis_index("lat")
    field = state[0]

    partner_state = to_partner(lax.dynamic_slice_in_dim(field, HALF * (1 - member), HALF, 1))

    table = lon_table()
    sent = forward(field.reshape(ROWS * LEVELS, NLON), jnp.asarray(table))
    gathered = over_lat(sent).reshape(NLAT, OWN * LEVELS)

    mix = jnp.where(member == 1, vertical_mix, jnp.roll(vertical_mix, HALF, axis=0))
    eye = jnp.eye(8, dtype=F32)
    spread = mix.T[:, None, :, None] * eye[None, :, None, :]
    for_noise = jnp.transpose(spread, (1, 0, 2, 3)).reshape(256, 256)
    spread = spread.reshape(256, 256)
    mix_high = spread.astype(BF16)
    mix_low = (spread - lax.reduce_precision(spread, 8, 7)).astype(BF16)
    pick = np.zeros((OWN, OWN * LEVELS), np.float32)
    n = np.arange(OWN * LEVELS)
    pick[8 * (n // 256) + n % 8, n] = math.sqrt(2.0 / NLAT) / math.sqrt(NLON)
    mixed_noise, wide_gain = prepare(
        noise[0].reshape(OWN * LEVELS, NK), for_noise, gain, jnp.asarray(pick)
    )

    high, low = lat_bases()
    bases = [high, low, high.transpose(0, 2, 1), low.transpose(0, 2, 1)]
    odd = (lat % 8 >= 4).astype(jnp.int32).reshape(1)
    give, keep = spectral(
        odd, gathered, [jnp.asarray(b) for b in bases], (mix_high, mix_low), mixed_noise, wide_gain
    )
    give = over_lat(give.reshape(LAT, ROWS, TILES * 128))
    partner_coef = to_partner(give)
    keep = over_lat(keep.reshape(LAT, ROWS, TILES * 128))

    back_table = jnp.asarray(np.ascontiguousarray(table.T))
    mine = member.astype(jnp.int32).reshape(1)
    new, skill_a = own_step(1 - mine, give, field, target, back_table)
    new, skill_b = own_step(mine, keep, field, target, back_table, new)
    part = other_step(mine, partner_coef, partner_state, new, back_table)
    rest = to_partner(part)
    crps = (skill_a + skill_b) * F32(1.0 / LEVELS) - (part + rest) * F32(0.5 / LEVELS)
    return new[None], crps[None]


def solution(mesh):
    placed = (
        P(("ic", "member"), "lat", None, None),
        P(("ic", "lat"), None, None),
        P(("ic", "member"), "lat", None, None),
        P("lat", None),
        P(),
    )
    return jax.shard_map(
        body,
        mesh=mesh,
        in_specs=placed,
        out_specs=(P(("ic", "member"), "lat", None, None), P(("ic", "member"), "lat", None)),
        check_vma=False,
    )
```

time: 448 us -> 140 us (0.31); the launches traced: 442 us -> 139 us
  local copies, waits for them, and re-layouts: 146 us -> 12.2 us
  matrix products: 107 us -> 0 us
  waiting for transfers between devices: 110 us -> 23.5 us
  Pallas kernels: 0 us -> 58.9 us
  blocking collectives: 40.3 us -> 19.6 us
  other arithmetic: 19.4 us -> 5.37 us
    dot_general x5 -> x0, matrix products: 107 us -> none  [the longest x1 36.2 us: body(): jnp.dot(field.reshape(rows * levels, NLON), table, preferred_element_type...]
    all_to_all x3 -> x2, waiting for transfers between devices: 110 us -> 2.91 us  [over_lat(): return lax.all_to_all(x, 'lat', split_axis=0, concat_axis=0, tiled=True)]
    pallas_call x0 -> x6, Pallas kernels: none -> 58.9 us  [the longest x2 20.2 us: own_step(): pl.pallas_call(own_kernel, grid_spec=pltpu.PrefetchScalarGridSpec(num_sca...]
    unnamed x11 -> x14, local copies, waits for them, and re-layouts: 54.4 us -> 2.96 us
    all_to_all x4 -> x0, local copies, waits for them, and re-layouts: 26 us -> none  [the longest x2 14.4 us: body(): lax.all_to_all(zonal, 'lat', split_axis=2, concat_axis=0, tiled=True)]
    reshape x3 -> x0, local copies, waits for them, and re-layouts: 25.2 us -> none  [the longest x1 9.17 us: body(): (zonal * jnp.float32(1.0 / math.sqrt(NLON))).reshape(rows, levels, 2 * MW)]
    all_to_all x2 -> x1, blocking collectives: 40.3 us -> 19.6 us  [over_lat(): return lax.all_to_all(x, 'lat', split_axis=0, concat_axis=0, tiled=True)]
    ppermute x0 -> x3, waiting for transfers between devices: none -> 20.5 us  [to_partner(): return lax.ppermute(x, 'member', [(0, 1), (1, 0)])]
  transfers between devices with their start and end apart: 3 -> 5, of which waited for: 3 -> 4; matrix products, arithmetic and copies ran while one was open for 1% -> 9% of each run, Pallas kernels for 0% -> 28%
where the time goes in v1:
time: 140 us; the launch traced here: 139 us
  Pallas kernels  58.9 us (42%)
  waiting for transfers between devices  23.5 us (17%)
  blocking collectives  19.6 us (14%)
  starting transfers between devices  18.9 us (13%)
  local copies, waits for them, and re-layouts  12.2 us (9%)
  other arithmetic  5.37 us (4%)
    ppermute x3, waiting for transfers between devices, to_partner(): return lax.ppermute(x, 'member', [(0, 1), (1, 0)])  20.5 us
    pallas_call x2, Pallas kernels, own_step(): pl.pallas_call(own_kernel, grid_spec=pltpu.PrefetchScalarGridSpec(num_sca...  20.2 us
    all_to_all x1, blocking collectives, over_lat(): return lax.all_to_all(x, 'lat', split_axis=0, concat_axis=0, tiled=True)  19.6 us
    pallas_call x1, Pallas kernels, spectral(): pl.pallas_call(spectral_kernel, grid_spec=pltpu.PrefetchScalarGridSpec(nu...  11.6 us
    pallas_call x1, Pallas kernels, forward(): pl.pallas_call(forward_kernel, grid=(GROUPS,), in_specs=[pl.BlockSpec((ro...  10.9 us
    all_to_all x2, starting transfers between devices, over_lat(): return lax.all_to_all(x, 'lat', split_axis=0, concat_axis=0, tiled=True)  10.8 us
    pallas_call x1, Pallas kernels, other_step(): pl.pallas_call(other_kernel, grid_spec=pltpu.PrefetchScalarGridSpec(num_s...  9.46 us
    ppermute x3, starting transfers between devices, to_partner(): return lax.ppermute(x, 'member', [(0, 1), (1, 0)])  8.07 us
  transfers between devices with their start and end apart: 5, of which 4 were waited for; matrix products, arithmetic and copies ran while one was open for 9% of the time, Pallas kernels for 28%

profile of v1, /device:TPU:0, one launch (start us, length us, event | category | flops | bytes accessed | tf_op | source)
XLA Modules:
  0.0 139.1 jit_solution(11870963196905636872)
XLA Ops:
  0.6 10.9 %forward_lon.1 = bf16[16,40,1280]{2,1,0:T(8,128)(2,1)} custom-call(bf16[1280,2560]{1,0:T(8,128)(2,1)} %bitcast.21, bf16[2560,640]{1,0:T(8,128)(2,1)} %constant.52.clone.table_ref), custom_call_target="tpu_custom_call" | custom-call | flops 4194304000 | bytes 12000000 | tf_op jit(solution)/shard_map/forward_lon/pallas_call | solution.py:88
  11.5 7.1 %all-to-all-start = ((bf16[16,40,1280]{2,1,0:T(8,128)(2,1)}), bf16[16,40,1280]{2,1,0:T(8,128)(2,1)S(1)}, u32[]{:S(2)}, u32[]{:S(2)}) async-start(bf16[16,40,1280]{2,1,0:T(8,128)(2,1)} %forward_lon.1), calls=%async_computation | async-start | bytes 3276800 | tf_op jit(solution)/shard_map/all_to_all | solution.py:289
  18.7 3.9 %dynamic-slice_bitcast_fusion = bf16[40,16,2560]{2,1,0:T(8,128)(2,1)} fusion(bf16[1,40,32,2560]{3,2,1,0:T(8,128)(2,1)} %param.12, s32[]{:T(128)S(6)} %select_n.21), kind=kLoop, calls=%fused_computation | loop fusion | bytes 6553604 | tf_op jit(solution)/shard_map/dynamic_slice | solution.py:297
  22.5 3.9 %collective-permute-start.1 = (bf16[40,16,2560]{2,1,0:T(8,128)(2,1)}, bf16[40,16,2560]{2,1,0:T(8,128)(2,1)}, u32[]{:S(2)}, u32[]{:S(2)}) collective-permute-start(bf16[40,16,2560]{2,1,0:T(8,128)(2,1)} %dynamic-slice_bitcast_fusion), channel_id=1, source_target_pairs={{0,16},{16,0},{1,17},{17,1},{2,18},{18,2},{3,19},{19,3},{4,20},{20... | collective-permute-start | bytes 9830408 | tf_op jit(solution)/shard_map/ppermute | solution.py:285
  27.1 0.8 copy.19.mix_ref
  27.9 2.6 %broadcast_multiply_fusion = f32[32,8,32,8]{3,2,1,0:T(8,128)} fusion(f32[8,8]{1,0:T(8,128)S(1)} %copy.18, f32[32,32]{1,0:T(8,128)S(1)} %copy.17), kind=kLoop, calls=%fused_computation.1 | loop fusion | flops 65536 | bytes 266496 | tf_op jit(solution)/shard_map/mul | solution.py:305
  30.5 4.0 %mul.43 = f32[256,256]{1,0:T(8,128)S(1)} reshape(f32[32,8,32,8]{3,2,1,0:T(8,128)} %broadcast_multiply_fusion) | data formatting | bytes 524288 | tf_op jit(solution)/shard_map/mul | solution.py:305
  34.6 6.8 %prepare_noise.1 = (f32[320,1280]{1,0:T(8,128)}, f32[320,1280]{1,0:T(8,128)}) custom-call(f32[1280,320]{1,0:T(8,128)} %bitcast.28, f32[256,256]{1,0:T(8,128)} %copy.19.mix_ref, f32[40,320]{1,0:T(8,128)} %gain_ref.1, f32[40,1280]{1,0:T(8,128)} %constant.53.clone.pick_ref), custom_call_target="tpu_custom_call" | custom-call | flops 1258291200 | bytes 6000000 | tf_op jit(solution)/shard_map/prepare_noise/pallas_call | solution.py:117
  42.1 1.2 all-to-all-done
  43.3 1.2 copy-done.2
  44.4 11.6 %spectral_step.1 = (bf16[640,640]{1,0:T(8,128)(2,1)}, bf16[640,640]{1,0:T(8,128)(2,1)}) custom-call(s32[1]{0:T(128)} %bitcast.1.odd, bf16[640,1280]{1,0:T(8,128)(2,1)} %bitcast.25, bf16[2,320,640]{2,1,0:T(8,128)(2,1)} %constant.54.clone.bh_ref, bf16[2,320,640]{2,1,0:T(8,128)(2,1)} %constant.55.clone.bl_ref, bf16[2,640,320]{2,1,0:T(8,128)(2,1)} %constant.56.clone.th_ref, ...), custom_call_target="tpu_custom_call" | custom-call | flops 4000000000 | bytes 10000000 | tf_op jit(solution)/shard_map/spectral_step/pallas_call | solution.py:166
  56.1 19.6 %all_to_all.15.coef_ref = bf16[16,40,640]{2,1,0:T(8,128)(2,1)S(1)} all-to-all(bf16[16,40,640]{2,1,0:T(8,128)(2,1)} %bitcast.27), channel_id=1, replica_groups=mesh['ic'=4,'member'=2,'lat'=16] {'lat'}, dimensions={0} | all-to-all | bytes 1638400 | tf_op jit(solution)/shard_map/all_to_all | solution.py:289
  75.7 3.6 %all-to-all-start.1 = ((bf16[16,40,640]{2,1,0:T(8,128)(2,1)}), bf16[16,40,640]{2,1,0:T(8,128)(2,1)S(1)}, u32[]{:S(2)}, u32[]{:S(2)}) async-start(bf16[16,40,640]{2,1,0:T(8,128)(2,1)} %bitcast.26), calls=%async_computation.1 | async-start | bytes 1638400 | tf_op jit(solution)/shard_map/all_to_all | solution.py:289
  79.3 0.9 collective-permute-start
  80.3 10.1 %own_step.2 = (bf16[40,32,2560]{2,1,0:T(8,128)(2,1)}, f32[40,2560]{1,0:T(8,128)}) custom-call(s32[1]{0:T(128)S(6)} %sub.13.where, bf16[16,40,640]{2,1,0:T(8,128)(2,1)} %copy-done, bf16[40,32,2560]{2,1,0:T(8,128)(2,1)} %bitcast.22, bf16[40,32,2560]{2,1,0:T(8,128)(2,1)} %target_ref.3, bf16[640,2560]{1,0:T(8,128)(2,1)} %constant.58.clone.table_ref), custom_call_target="tpu_custom_call" | custom-call | flops 2097152000 | bytes 14000000 | tf_op jit(solution)/shard_map/own_step/pallas_call | solution.py:223
  90.4 1.7 %all-to-all-done.1.coef_ref = bf16[16,40,640]{2,1,0:T(8,128)(2,1)S(1)} async-done(((bf16[16,40,640]{2,1,0:T(8,128)(2,1)}), bf16[16,40,640]{2,1,0:T(8,128)(2,1)S(1)}, u32[]{:S(2)}, u32[]{:S(2)}) %all-to-all-start.1) | async-done | bytes 819232 | tf_op jit(solution)/shard_map/all_to_all | solution.py:289
  92.1 0.9 copy-done.1
  93.0 10.1 %own_step.3 = (bf16[40,32,2560]{2,1,0:T(8,128)(2,1)}, f32[40,2560]{1,0:T(8,128)}) custom-call(s32[1]{0:T(128)} %bitcast.where, bf16[16,40,640]{2,1,0:T(8,128)(2,1)} %copy-done.1, bf16[40,32,2560]{2,1,0:T(8,128)(2,1)} %bitcast.23, bf16[40,32,2560]{2,1,0:T(8,128)(2,1)} %target_ref.3, ...), custom_call_target="tpu_custom_call", output_to_operand_aliasing={{0}: (5, {})} | custom-call | flops 2097152000 | bytes 14000000 | tf_op jit(solution)/shard_map/own_step/pallas_call | solution.py:223
  103.1 11.7 %collective-permute-done.coef_ref = bf16[16,40,640]{2,1,0:T(8,128)(2,1)S(1)} collective-permute-done((bf16[16,40,640]{2,1,0:T(8,128)(2,1)S(1)}, bf16[16,40,640]{2,1,0:T(8,128)(2,1)S(1)}, u32[]{:S(2)}, u32[]{:S(2)}) %collective-permute-start) | collective-permute-done | bytes 819232 | tf_op jit(solution)/shard_map/ppermute | solution.py:285
  114.8 0.9 copy-done.3
  115.7 9.5 %other_step.1 = f32[40,2560]{1,0:T(8,128)} custom-call(s32[1]{0:T(128)} %bitcast.where, bf16[16,40,640]{2,1,0:T(8,128)(2,1)} %copy-done.3, bf16[40,16,2560]{2,1,0:T(8,128)(2,1)} %collective-permute-done.1.state_ref, bf16[40,32,2560]{2,1,0:T(8,128)(2,1)} %get-tuple-element.15.own_ref, bf16[640,2560]{1,0:T(8,128)(2,1)} %constant.58.clone.table_ref), custom_call_target="tpu_custom_call" | custom-call | flops 2097152000 | bytes 12000000 | tf_op jit(solution)/shard_map/other_step/pallas_call | solution.py:262
  125.2 3.2 %collective-permute-start.2 = (f32[40,2560]{1,0:T(8,128)}, f32[40,2560]{1,0:T(8,128)S(1)}, u32[]{:S(2)}, u32[]{:S(2)}) collective-permute-start(f32[40,2560]{1,0:T(8,128)} %other_step.1), channel_id=1, source_target_pairs={{0,16},{16,0},{1,17},{17,1},{2,18},{18,2},{3,19},{19,3},{4,20},{20... | collective-permute-start | bytes 1228808 | tf_op jit(solution)/shard_map/ppermute | solution.py:285
  128.4 8.8 %collective-permute-done.2 = f32[40,2560]{1,0:T(8,128)S(1)} collective-permute-done((f32[40,2560]{1,0:T(8,128)}, f32[40,2560]{1,0:T(8,128)S(1)}, u32[]{:S(2)}, u32[]{:S(2)}) %collective-permute-start.2) | collective-permute-done | bytes 409632 | tf_op jit(solution)/shard_map/ppermute | solution.py:285
  137.3 1.8 %subtract_bitcast_fusion = f32[1,40,2560]{2,1,0:T(8,128)} fusion(f32[40,2560]{1,0:T(8,128)} %other_step.1, f32[40,2560]{1,0:T(8,128)S(1)} %collective-permute-done.2, f32[40,2560]{1,0:T(8,128)S(1)} %copy-done.4, f32[40,2560]{1,0:T(8,128)S(1)} %copy-done.5), kind=kLoop, calls=%fused_computation.3 | loop fusion | flops 512000 | bytes 2048000 | tf_op jit(solution)/shard_map/broadcast_in_dim | solution.py:334
  (20 shorter events, 1.4 us)
Async XLA Ops:
  11.5 31.8 %all-to-all-start = ((bf16[16,40,1280]{2,1,0:T(8,128)(2,1)}), bf16[16,40,1280]{2,1,0:T(8,128)(2,1)S(1)}, u32[]{:S(2)}, u32[]{:S(2)}) async-start(bf16[16,40,1280]{2,1,0:T(8,128)(2,1)} %forward_lon.1), calls=%async_computation | async-start | bytes 3276800 | tf_op jit(solution)/shard_map/all_to_all | solution.py:289
  18.7 7.8 %copy-start.6 = (f32[32,32]{1,0:T(8,128)S(1)}, f32[32,32]{1,0:T(8,128)}, u32[]{:S(2)}) copy-start(f32[32,32]{1,0:T(8,128)} %param.16) | copy-start | bytes 12292
  22.5 92.3 %collective-permute-start.1 = (bf16[40,16,2560]{2,1,0:T(8,128)(2,1)}, bf16[40,16,2560]{2,1,0:T(8,128)(2,1)}, u32[]{:S(2)}, u32[]{:S(2)}) collective-permute-start(bf16[40,16,2560]{2,1,0:T(8,128)(2,1)} %dynamic-slice_bitcast_fusion), channel_id=1, source_target_pairs={{0,16},{16,0},{1,17},{17,1},{2,18},{18,2},{3,19},{19,3},{4,20},{20... | collective-permute-start | bytes 9830408 | tf_op jit(solution)/shard_map/ppermute | solution.py:285
  43.3 1.2 copy-start.2
  75.7 4.6 %copy-start = (bf16[16,40,640]{2,1,0:T(8,128)(2,1)}, bf16[16,40,640]{2,1,0:T(8,128)(2,1)S(1)}, u32[]{:S(2)}) copy-start(bf16[16,40,640]{2,1,0:T(8,128)(2,1)S(1)} %all_to_all.15.coef_ref) | copy-start | bytes 2457604
  75.7 16.4 %all-to-all-start.1 = ((bf16[16,40,640]{2,1,0:T(8,128)(2,1)}), bf16[16,40,640]{2,1,0:T(8,128)(2,1)S(1)}, u32[]{:S(2)}, u32[]{:S(2)}) async-start(bf16[16,40,640]{2,1,0:T(8,128)(2,1)} %bitcast.26), calls=%async_computation.1 | async-start | bytes 1638400 | tf_op jit(solution)/shard_map/all_to_all | solution.py:289
  79.3 35.5 %collective-permute-start = (bf16[16,40,640]{2,1,0:T(8,128)(2,1)S(1)}, bf16[16,40,640]{2,1,0:T(8,128)(2,1)S(1)}, u32[]{:S(2)}, u32[]{:S(2)}) collective-permute-start(bf16[16,40,640]{2,1,0:T(8,128)(2,1)S(1)} %all_to_all.15.coef_ref), channel_id=1, source_target_pairs={{0,16},{16,0},{1,17},{17,1},{2,18},{18,2},{3,19},{19,3},{4,20},{20... | collective-permute-start | bytes 2457608 | tf_op jit(solution)/shard_map/ppermute | solution.py:285
  92.1 0.9 copy-start.1
  114.8 0.9 copy-start.3
  115.7 21.5 %copy-start.4 = (f32[40,2560]{1,0:T(8,128)S(1)}, f32[40,2560]{1,0:T(8,128)}, u32[]{:S(2)}) copy-start(f32[40,2560]{1,0:T(8,128)} %get-tuple-element.16) | copy-start | bytes 1228804
  115.7 21.5 %copy-start.5 = (f32[40,2560]{1,0:T(8,128)S(1)}, f32[40,2560]{1,0:T(8,128)}, u32[]{:S(2)}) copy-start(f32[40,2560]{1,0:T(8,128)} %get-tuple-element.17) | copy-start | bytes 1228804
  125.2 12.1 %collective-permute-start.2 = (f32[40,2560]{1,0:T(8,128)}, f32[40,2560]{1,0:T(8,128)S(1)}, u32[]{:S(2)}, u32[]{:S(2)}) collective-permute-start(f32[40,2560]{1,0:T(8,128)} %other_step.1), channel_id=1, source_target_pairs={{0,16},{16,0},{1,17},{17,1},{2,18},{18,2},{3,19},{19,3},{4,20},{20... | collective-permute-start | bytes 1228808 | tf_op jit(solution)/shard_map/ppermute | solution.py:285

commit v2 on v1

v2 whole, which is shorter than its diff:
```python
import math

import jax
import jax.numpy as jnp
import ml_dtypes
import numpy as np
from jax import lax
from jax.experimental import pallas as pl
from jax.experimental.pallas import tpu as pltpu
from jax.sharding import PartitionSpec as P


NLON = 2560
NLAT = 640
MW = 320
LEVELS = 32
NK = 320
NCOL = 2 * MW
LAT = 16
ROWS = NLAT // LAT
OWN = NCOL // LAT
HALF = LEVELS // 2
TILES = OWN // 8
GROUPS = ROWS // 8
BF16 = jnp.bfloat16
F32 = jnp.float32
HIGHEST = lax.Precision.HIGHEST
OWN_LIMIT = 58 << 20
SMALL_LIMIT = 16 << 20
HBM = pl.BlockSpec(memory_space=pltpu.HBM)
VMEM = pl.BlockSpec(memory_space=pltpu.VMEM)
SMEM = pl.BlockSpec(memory_space=pltpu.SMEM)
FIELD = (ROWS, HALF, NLON)


def column_order():
    n = np.arange(NCOL)
    return 40 * ((n % 128) // 8) + 8 * (n // 128) + n % 8


def lon_table():
    column = column_order()
    part = column // MW
    rest = column % MW
    half = MW // 2
    wave = np.where(rest < half, 2 * rest + 2 * part, 2 * (rest - half) + 1)
    phase = np.arange(NLON)[:, None] * wave[None, :] % NLON
    angle = 2.0 * math.pi / NLON * phase
    table = np.where(part[None, :] == 0, np.cos(angle), np.sin(angle))
    return table.astype(np.float32).astype(ml_dtypes.bfloat16)


def lat_bases():
    theta = (np.arange(NLAT) + 0.5) * (math.pi / NLAT)
    modes = np.arange(NK)
    even = np.cos(modes[:, None] * theta[None, :])
    odd = np.sin((modes[:, None] + 1.0) * theta[None, :])
    both = np.stack([even, odd]).astype(np.float32)
    high = both.astype(ml_dtypes.bfloat16)
    low = (both - high.astype(np.float32)).astype(ml_dtypes.bfloat16)
    return high, low


def turn(x, groups):
    return pltpu.roll(x, 8 * groups % 128, 1) if groups % 16 else x


def swap_groups(v):
    group = lax.broadcasted_iota(jnp.int32, v[0].shape, 1) // 8
    x = [turn(v[-b % 16], -b % 16) for b in range(16)]
    for bit in range(4):
        moved = (group & (1 << bit)) != 0
        x = [jnp.where(moved, x[(g - (1 << bit)) % 16], x[g]) for g in range(16)]
    return [turn(x[g], 16 - g) for g in range(16)]


def forward_kernel(x_ref, table_ref, out_ref, held):
    step = pl.program_id(0)
    now, before = lax.rem(step, 2), lax.rem(step + 1, 2)
    zonal = jnp.dot(x_ref[...], table_ref[...], preferred_element_type=F32)
    for t in range(TILES):
        for h in range(2):
            v = [held[before, t, pl.ds(HALF * h + a, 8, stride=40), :] for a in range(16)]
            lanes = slice(128 * (2 * t + h), 128 * (2 * t + h + 1))
            for q, w in enumerate(swap_groups(v)):
                out_ref[q, :, lanes] = w.astype(BF16)
    for t in range(TILES):
        for j in range(8):
            held[now, t, 40 * j : 40 * j + 32, :] = zonal[
                32 * j : 32 * j + 32, 128 * t : 128 * (t + 1)
            ]


def forward(field, table):
    rows = field.shape[0]
    return pl.pallas_call(
        forward_kernel,
        grid=(GROUPS + 1,),
        in_specs=[
            pl.BlockSpec((rows // GROUPS, NLON), lambda i: (jnp.minimum(i, GROUPS - 1), 0)),
            pl.BlockSpec((NLON, NCOL), lambda i: (0, 0)),
        ],
        out_specs=pl.BlockSpec((LAT, 8, OWN * LEVELS), lambda i: (0, jnp.maximum(i - 1, 0), 0)),
        out_shape=jax.ShapeDtypeStruct((LAT, ROWS, OWN * LEVELS), BF16),
        scratch_shapes=[pltpu.VMEM((2, TILES, 8 * 40, 128), F32)],
        cost_estimate=pl.CostEstimate(
            flops=2 * rows * NLON * NCOL, bytes_accessed=12_000_000, transcendentals=0
        ),
        compiler_params=pltpu.CompilerParams(vmem_limit_bytes=SMALL_LIMIT),
        name="forward_lon",
    )(field, table)


def prepare_kernel(noise_ref, mix_ref, gain_ref, pick_ref, mixed_ref, wide_ref):
    contract = (((0,), (0,)), ((), ()))
    mixed_ref[...] = lax.dot_general(
        noise_ref[...], mix_ref[...], contract, precision=HIGHEST, preferred_element_type=F32
    )
    wide_ref[...] = lax.dot_general(
        gain_ref[...], pick_ref[...], contract, precision=HIGHEST, preferred_element_type=F32
    )


def prepare(noise, mix, gain, pick):
    wide = OWN * LEVELS
    return pl.pallas_call(
        prepare_kernel,
        grid=(TILES,),
        in_specs=[
            pl.BlockSpec((256, NK), lambda t: (t, 0)),
            pl.BlockSpec((256, 256), lambda t: (0, 0)),
            pl.BlockSpec((OWN, NK), lambda t: (0, 0)),
            pl.BlockSpec((OWN, 256), lambda t: (0, t)),
        ],
        out_specs=[
            pl.BlockSpec((NK, 256), lambda t: (0, t)),
            pl.BlockSpec((NK, 256), lambda t: (0, t)),
        ],
        out_shape=[jax.ShapeDtypeStruct((NK, wide), F32)] * 2,
        cost_estimate=pl.CostEstimate(
            flops=12 * 256 * NK * wide, bytes_accessed=6_000_000, transcendentals=0
        ),
        compiler_params=pltpu.CompilerParams(vmem_limit_bytes=SMALL_LIMIT),
        name="prepare_noise",
    )(noise, mix, gain, pick)


def halves(x):
    high = x.astype(BF16)
    return high, (x - high.astype(F32)).astype(BF16)


def mm(a, b):
    return jnp.dot(a, b, preferred_element_type=F32)


def spectral_kernel(odd, g_ref, b_ref, t_ref, mh_ref, ml_ref, noise_ref, gain_ref, send_ref, keep_ref, b, t, noise, gain, sems):
    loads = [
        pltpu.make_async_copy(b_ref.at[odd[0]], b, sems.at[0]),
        pltpu.make_async_copy(gain_ref, gain, sems.at[1]),
        pltpu.make_async_copy(noise_ref, noise, sems.at[2]),
        pltpu.make_async_copy(t_ref.at[odd[0]], t, sems.at[3]),
    ]
    for copy in loads:
        copy.start()
    loads[0].wait()
    for k in range(TILES):
        lanes = slice(256 * k, 256 * (k + 1))
        both = mm(b[...], g_ref[:, lanes])
        if k == 0:
            loads[1].wait()
        forced = (both[:NK] + both[NK:]) * gain[:, lanes]
        high, low = halves(forced)
        both = mm(jnp.concatenate([high, low], axis=0), mh_ref[...])
        if k == 0:
            loads[2].wait()
        mixed = both[:NK] + both[NK:] + mm(high, ml_ref[...]) + noise[:, lanes]
        high, low = halves(mixed)
        if k == 0:
            loads[3].wait()
        both = mm(t[...], high)
        back = both[:NLAT] + both[NLAT:] + mm(t[:NLAT], low)
        back = (back * F32(math.sqrt(2.0) / NK)).astype(BF16)
        send_ref[:, 128 * k : 128 * (k + 1)] = back[:, :128]
        keep_ref[:, 128 * k : 128 * (k + 1)] = back[:, 128:]


def spectral(odd, gathered, bases, mixes, noise, gain):
    return pl.pallas_call(
        spectral_kernel,
        in_specs=[SMEM, VMEM, HBM, HBM, VMEM, VMEM, HBM, HBM],
        out_specs=[VMEM, VMEM],
        out_shape=[jax.ShapeDtypeStruct((NLAT, TILES * 128), BF16)] * 2,
        scratch_shapes=[
            pltpu.VMEM((2 * NK, NLAT), BF16),
            pltpu.VMEM((2 * NLAT, NK), BF16),
            pltpu.VMEM((NK, OWN * LEVELS), F32),
            pltpu.VMEM((NK, OWN * LEVELS), F32),
            pltpu.SemaphoreType.DMA((4,)),
        ],
        cost_estimate=pl.CostEstimate(
            flops=4_000_000_000, bytes_accessed=10_000_000, transcendentals=0
        ),
        compiler_params=pltpu.CompilerParams(vmem_limit_bytes=OWN_LIMIT),
        name="spectral_step",
    )(odd, gathered, *bases, *mixes, noise, gain)


def set_rows(coef_ref, held, rows_ref, groups):
    for i in groups:
        for t in range(TILES):
            lanes = slice(128 * t, 128 * (t + 1))
            v = [coef_ref[q, 8 * i : 8 * i + 8, lanes].astype(F32) for q in range(LAT)]
            for a, w in enumerate(swap_groups(v)):
                held[TILES * i + t, pl.ds(a, 8, stride=24), :] = w
    for j in range(8 * groups[0], 8 * groups[-1] + 8):
        for t in range(TILES):
            k = 24 * (j % 8)
            level = held[TILES * (j // 8) + t, k : k + 16, :].astype(BF16)
            rows_ref[HALF * j : HALF * (j + 1), 128 * t : 128 * (t + 1)] = level


CHUNK = 512


def updated(rows, table, state):
    return (state.astype(F32) + mm(rows, table).reshape(state.shape)).astype(BF16)


def distance(a, b):
    return jnp.sum(jnp.abs(a.astype(F32) - b.astype(F32)), axis=1)


BLOCKS = [range(0, 3), range(3, GROUPS)]


def own_kernel(where, coef_ref, state_ref, target_ref, table, *rest):
    new_ref, new, skill_ref, held, rows_ref, state, target, sems = rest[-8:]
    levels = pl.ds(pl.multiple_of(HALF * where[0], HALF), HALF)
    loads, stores = [], []
    for k, groups in enumerate(BLOCKS):
        rows = slice(8 * groups[0], 8 * groups[-1] + 8)
        loads.append([
            pltpu.make_async_copy(state_ref.at[rows, levels], state.at[rows], sems.at[0, k]),
            pltpu.make_async_copy(target_ref.at[rows, levels], target.at[rows], sems.at[1, k]),
        ])
        stores.append(
            pltpu.make_async_copy(new.at[rows], new_ref.at[rows, levels], sems.at[2, k])
        )
        for copy in loads[-1]:
            copy.start()
    for k, groups in enumerate(BLOCKS):
        rows = slice(8 * groups[0], 8 * groups[-1] + 8)
        set_rows(coef_ref, held, rows_ref, groups)
        for copy in loads[k]:
            copy.wait()
        for n in range(0, NLON, CHUNK):
            cut = slice(n, n + CHUNK)
            block = rows_ref[HALF * rows.start : HALF * rows.stop]
            value = updated(block, table[:, cut], state[rows, :, cut])
            new[rows, :, cut] = value
            skill_ref[rows, cut] = distance(value, target[rows, :, cut])
        stores[k].start()
    for store in stores:
        store.wait()


def own_step(where, coef, state, target, table, *into):
    return pl.pallas_call(
        own_kernel,
        in_specs=[SMEM, VMEM, HBM, HBM, VMEM] + [HBM for _ in into],
        out_specs=[HBM, VMEM, VMEM],
        out_shape=[
            jax.ShapeDtypeStruct((ROWS, LEVELS, NLON), BF16),
            jax.ShapeDtypeStruct(FIELD, BF16),
            jax.ShapeDtypeStruct((ROWS, NLON), F32),
        ],
        scratch_shapes=[
            pltpu.VMEM((GROUPS * TILES, 8 * 24, 128), F32),
            pltpu.VMEM((ROWS * HALF, NCOL), BF16),
            pltpu.VMEM(FIELD, BF16),
            pltpu.VMEM(FIELD, BF16),
            pltpu.SemaphoreType.DMA((3, 2)),
        ],
        input_output_aliases={5: 0} if into else {},
        cost_estimate=pl.CostEstimate(
            flops=2 * ROWS * HALF * NCOL * NLON, bytes_accessed=14_000_000, transcendentals=0
        ),
        compiler_params=pltpu.CompilerParams(vmem_limit_bytes=OWN_LIMIT),
        name="own_step",
    )(where, coef, state, target, table, *into)


def other_kernel(coef_ref, state_ref, own, table, part_ref, held, rows_ref, state, sems):
    loads = []
    for k, groups in enumerate(BLOCKS):
        rows = slice(8 * groups[0], 8 * groups[-1] + 8)
        loads.append(pltpu.make_async_copy(state_ref.at[rows], state.at[rows], sems.at[k]))
        loads[-1].start()
    for k, groups in enumerate(BLOCKS):
        rows = slice(8 * groups[0], 8 * groups[-1] + 8)
        set_rows(coef_ref, held, rows_ref, groups)
        loads[k].wait()
        for n in range(0, NLON, CHUNK):
            cut = slice(n, n + CHUNK)
            block = rows_ref[HALF * rows.start : HALF * rows.stop]
            value = updated(block, table[:, cut], state[rows, :, cut])
            part_ref[rows, cut] = distance(value, own[rows, :, cut])


def other_step(*operands):
    return pl.pallas_call(
        other_kernel,
        in_specs=[VMEM, HBM, VMEM, VMEM],
        out_specs=VMEM,
        out_shape=jax.ShapeDtypeStruct((ROWS, NLON), F32),
        scratch_shapes=[
            pltpu.VMEM((GROUPS * TILES, 8 * 24, 128), F32),
            pltpu.VMEM((ROWS * HALF, NCOL), BF16),
            pltpu.VMEM(FIELD, BF16),
            pltpu.SemaphoreType.DMA((2,)),
        ],
        cost_estimate=pl.CostEstimate(
            flops=2 * ROWS * HALF * NCOL * NLON, bytes_accessed=12_000_000, transcendentals=0
        ),
        compiler_params=pltpu.CompilerParams(vmem_limit_bytes=SMALL_LIMIT),
        name="other_step",
    )(*operands)


def to_partner(x):
    return lax.ppermute(x, "member", [(0, 1), (1, 0)])


def over_lat(x):
    return lax.all_to_all(x, "lat", split_axis=0, concat_axis=0, tiled=True)


def body(state, target, noise, gain, vertical_mix):
    member = lax.axis_index("member")
    lat = lax.axis_index("lat")
    field = state[0]

    partner_state = to_partner(lax.dynamic_slice_in_dim(field, HALF * (1 - member), HALF, 1))

    table = lon_table()
    sent = forward(field.reshape(ROWS * LEVELS, NLON), jnp.asarray(table))
    gathered = over_lat(sent).reshape(NLAT, OWN * LEVELS)

    mix = jnp.where(member == 1, vertical_mix, jnp.roll(vertical_mix, HALF, axis=0))
    eye = jnp.eye(8, dtype=F32)
    spread = mix.T[:, None, :, None] * eye[None, :, None, :]
    for_noise = jnp.transpose(spread, (1, 0, 2, 3)).reshape(256, 256)
    spread = spread.reshape(256, 256)
    mix_high = spread.astype(BF16)
    mix_low = (spread - lax.reduce_precision(spread, 8, 7)).astype(BF16)
    pick = np.zeros((OWN, OWN * LEVELS), np.float32)
    n = np.arange(OWN * LEVELS)
    pick[8 * (n // 256) + n % 8, n] = math.sqrt(2.0 / NLAT) / math.sqrt(NLON)
    mixed_noise, wide_gain = prepare(
        noise[0].reshape(OWN * LEVELS, NK), for_noise, gain, jnp.asarray(pick)
    )

    high, low = lat_bases()
    bases = [
        np.concatenate([high, low], axis=1),
        np.concatenate([high.transpose(0, 2, 1), low.transpose(0, 2, 1)], axis=1),
    ]
    odd = (lat % 8 >= 4).astype(jnp.int32).reshape(1)
    give, keep = spectral(
        odd, gathered, [jnp.asarray(b) for b in bases], (mix_high, mix_low), mixed_noise, wide_gain
    )
    give = over_lat(give.reshape(LAT, ROWS, TILES * 128))
    partner_coef = to_partner(give)
    keep = over_lat(keep.reshape(LAT, ROWS, TILES * 128))

    back_table = jnp.asarray(np.ascontiguousarray(table.T))
    mine = member.astype(jnp.int32).reshape(1)
    new, _, skill_a = own_step(1 - mine, give, field, target, back_table)
    new, own_half, skill_b = own_step(mine, keep, field, target, back_table, new)
    part = other_step(partner_coef, partner_state, own_half, back_table)
    rest = to_partner(part.astype(BF16)).astype(F32)
    base = (skill_a + skill_b) * F32(1.0 / LEVELS) - part * F32(0.5 / LEVELS)
    crps = lax.optimization_barrier(base) - rest * F32(0.5 / LEVELS)
    return new[None], crps[None]


def solution(mesh):
    placed = (
        P(("ic", "member"), "lat", None, None),
        P(("ic", "lat"), None, None),
        P(("ic", "member"), "lat", None, None),
        P("lat", None),
        P(),
    )

    return jax.shard_map(
        body,
        mesh=mesh,
        in_specs=placed,
        out_specs=(P(("ic", "member"), "lat", None, None), P(("ic", "member"), "lat", None)),
        check_vma=False,
    )
```

time: 140 us -> 133 us (0.950)
  local copies, waits for them, and re-layouts: 12.2 us -> 18.6 us
  Pallas kernels: 58.9 us -> 52.7 us
  waiting for transfers between devices: 23.5 us -> 17.4 us
    unnamed x14 -> x28, local copies, waits for them, and re-layouts: 2.96 us -> 9.96 us
    ppermute x3, waiting for transfers between devices: 20.5 us -> 15.3 us  [to_partner(): return lax.ppermute(x, 'member', [(0, 1), (1, 0)])]
    pallas_call x5, Pallas kernels: 52.1 us -> 48.7 us  [the longest x2 25.1 us: own_step(): pl.pallas_call(own_kernel, in_specs=[SMEM, VMEM, HBM, HBM, VMEM] + [HBM f...]
    pallas_call x1, Pallas kernels: 6.76 us -> 4.05 us  [prepare(): pl.pallas_call(prepare_kernel, grid=(TILES,), in_specs=[pl.BlockSpec((256...]
  transfers between devices with their start and end apart: 5 -> 5, of which waited for: 4 -> 3; matrix products, arithmetic and copies ran while one was open for 9% -> 9% of each run, Pallas kernels for 28% -> 29%
where the time goes in v2:
time: 133 us
  Pallas kernels  52.7 us (40%)
  starting transfers between devices  20.1 us (15%)
  blocking collectives  18.7 us (14%)
  local copies, waits for them, and re-layouts  18.6 us (14%)
  waiting for transfers between devices  17.4 us (13%)
  other arithmetic  4.42 us (3%)
    pallas_call x2, Pallas kernels, own_step(): pl.pallas_call(own_kernel, in_specs=[SMEM, VMEM, HBM, HBM, VMEM] + [HBM f...  25.1 us
    all_to_all x1, blocking collectives, over_lat(): return lax.all_to_all(x, 'lat', split_axis=0, concat_axis=0, tiled=True)  18.7 us
    ppermute x3, waiting for transfers between devices, to_partner(): return lax.ppermute(x, 'member', [(0, 1), (1, 0)])  15.3 us
    all_to_all x2, starting transfers between devices, over_lat(): return lax.all_to_all(x, 'lat', split_axis=0, concat_axis=0, tiled=True)  10.8 us
    unnamed x28, local copies, waits for them, and re-layouts  9.96 us
    pallas_call x1, Pallas kernels, spectral(): pl.pallas_call(spectral_kernel, in_specs=[SMEM, VMEM, HBM, HBM, VMEM, VME...  9.9 us
    ppermute x3, starting transfers between devices, to_partner(): return lax.ppermute(x, 'member', [(0, 1), (1, 0)])  9.27 us
    pallas_call x1, Pallas kernels, forward(): pl.pallas_call(forward_kernel, grid=(GROUPS + 1,), in_specs=[pl.BlockSpec...  8.14 us
  transfers between devices with their start and end apart: 5, of which 3 were waited for; matrix products, arithmetic and copies ran while one was open for 9% of the time, Pallas kernels for 29%

profile of v2, /device:TPU:0, one launch (start us, length us, event | category | flops | bytes accessed | tf_op | source)
XLA Modules:
  0.0 132.8 jit_solution(15347292172593220831)
XLA Ops:
  0.6 2.9 %copy-done = bf16[1,40,32,2560]{3,2,1,0:T(8,128)(2,1)S(1)} copy-done((bf16[1,40,32,2560]{3,2,1,0:T(8,128)(2,1)S(1)}, bf16[1,40,32,2560]{3,2,1,0:T(8,128)(2,1)}, u32[]{:S(2)}) %copy-start) | copy-done | bytes 6553624
  3.5 1.9 %copy-done.5 = bf16[2560,640]{1,0:T(8,128)(2,1)S(1)} copy-done((bf16[2560,640]{1,0:T(8,128)(2,1)S(1)}, bf16[2560,640]{1,0:T(8,128)(2,1)}, u32[]{:S(2)}) %copy-start.5) | copy-done | bytes 3276824
  5.4 8.1 %forward_lon.1 = bf16[16,40,1280]{2,1,0:T(8,128)(2,1)} custom-call(bf16[1280,2560]{1,0:T(8,128)(2,1)S(1)} %bitcast.23, bf16[2560,640]{1,0:T(8,128)(2,1)S(1)} %copy-done.5), custom_call_target="tpu_custom_call" | custom-call | flops 4194304000 | bytes 12000000 | tf_op jit(solution)/shard_map/forward_lon/pallas_call | solution.py:96
  13.6 7.2 %all-to-all-start = ((bf16[16,40,1280]{2,1,0:T(8,128)(2,1)}), bf16[16,40,1280]{2,1,0:T(8,128)(2,1)}, u32[]{:S(2)}, u32[]{:S(2)}) async-start(bf16[16,40,1280]{2,1,0:T(8,128)(2,1)} %forward_lon.1), calls=%async_computation | async-start | bytes 3276800 | tf_op jit(solution)/shard_map/all_to_all | solution.py:336
  20.8 3.9 %dynamic-slice_bitcast_fusion = bf16[40,16,2560]{2,1,0:T(8,128)(2,1)} fusion(bf16[1,40,32,2560]{3,2,1,0:T(8,128)(2,1)} %param.10, s32[]{:T(128)S(6)} %select_n.21), kind=kLoop, calls=%fused_computation | loop fusion | bytes 6553604 | tf_op jit(solution)/shard_map/dynamic_slice | solution.py:344
  24.7 3.9 %collective-permute-start.1 = (bf16[40,16,2560]{2,1,0:T(8,128)(2,1)}, bf16[40,16,2560]{2,1,0:T(8,128)(2,1)}, u32[]{:S(2)}, u32[]{:S(2)}) collective-permute-start(bf16[40,16,2560]{2,1,0:T(8,128)(2,1)} %dynamic-slice_bitcast_fusion), channel_id=1, source_target_pairs={{0,16},{16,0},{1,17},{17,1},{2,18},{18,2},{3,19},{19,3},{4,20},{20... | collective-permute-start | bytes 9830408 | tf_op jit(solution)/shard_map/ppermute | solution.py:332
  29.4 2.6 %broadcast_multiply_fusion = f32[32,8,32,8]{3,2,1,0:T(8,128)} fusion(f32[8,8]{1,0:T(8,128)S(1)} %copy.16, f32[32,32]{1,0:T(8,128)S(1)} %copy.15), kind=kLoop, calls=%fused_computation.1 | loop fusion | flops 65536 | bytes 266496 | tf_op jit(solution)/shard_map/mul | solution.py:352
  32.0 4.2 %mul.43 = f32[256,256]{1,0:T(8,128)S(1)} reshape(f32[32,8,32,8]{3,2,1,0:T(8,128)} %broadcast_multiply_fusion) | data formatting | bytes 524288 | tf_op jit(solution)/shard_map/mul | solution.py:352
  36.2 4.1 %prepare_noise.1 = (f32[320,1280]{1,0:T(8,128)S(1)}, f32[320,1280]{1,0:T(8,128)S(1)}) custom-call(f32[1280,320]{1,0:T(8,128)S(1)} %bitcast.24, f32[256,256]{1,0:T(8,128)S(1)} %copy.17.mix_ref, f32[40,320]{1,0:T(8,128)S(1)} %copy-done.4, f32[40,1280]{1,0:T(8,128)S(1)} %copy-done.6), custom_call_target="tpu_custom_call" | custom-call | flops 1258291200 | bytes 6000000 | tf_op jit(solution)/shard_map/prepare_noise/pallas_call | solution.py:126
  40.3 1.2 copy-done.7
  41.4 1.2 copy-done.8
  43.3 2.1 %all-to-all-done = bf16[16,40,1280]{2,1,0:T(8,128)(2,1)} async-done(((bf16[16,40,1280]{2,1,0:T(8,128)(2,1)}), bf16[16,40,1280]{2,1,0:T(8,128)(2,1)}, u32[]{:S(2)}, u32[]{:S(2)}) %all-to-all-start) | async-done | bytes 1638432 | tf_op jit(solution)/shard_map/all_to_all | solution.py:336
  45.4 9.9 %spectral_step.1 = (bf16[640,640]{1,0:T(8,128)(2,1)}, bf16[640,640]{1,0:T(8,128)(2,1)}) custom-call(s32[1]{0:T(128)} %bitcast.1.odd, bf16[640,1280]{1,0:T(8,128)(2,1)} %bitcast.3.g_ref, bf16[2,640,640]{2,1,0:T(8,128)(2,1)} %constant.50.clone.b_ref, bf16[2,1280,320]{2,1,0:T(8,128)(2,1)} %constant.51.clone.t_ref, bf16[256,256]{1,0:T(8,128)(2,1)} %get-tuple-element.23.mh_ref, ...), custom_call_target="tpu_custom_call" | custom-call | flops 4000000000 | bytes 10000000 | tf_op jit(solution)/shard_map/spectral_step/pallas_call | solution.py:189
  55.3 18.7 %all_to_all.15.coef_ref = bf16[16,40,640]{2,1,0:T(8,128)(2,1)S(1)} all-to-all(bf16[16,40,640]{2,1,0:T(8,128)(2,1)} %bitcast.27), channel_id=1, replica_groups=mesh['ic'=4,'member'=2,'lat'=16] {'lat'}, dimensions={0} | all-to-all | bytes 1638400 | tf_op jit(solution)/shard_map/all_to_all | solution.py:336
  74.0 3.6 %all-to-all-start.1 = ((bf16[16,40,640]{2,1,0:T(8,128)(2,1)}), bf16[16,40,640]{2,1,0:T(8,128)(2,1)S(1)}, u32[]{:S(2)}, u32[]{:S(2)}) async-start(bf16[16,40,640]{2,1,0:T(8,128)(2,1)} %bitcast.26), calls=%async_computation.1 | async-start | bytes 1638400 | tf_op jit(solution)/shard_map/all_to_all | solution.py:336
  77.7 2.1 %collective-permute-start = (bf16[16,40,640]{2,1,0:T(8,128)(2,1)S(1)}, bf16[16,40,640]{2,1,0:T(8,128)(2,1)S(1)}, u32[]{:S(2)}, u32[]{:S(2)}) collective-permute-start(bf16[16,40,640]{2,1,0:T(8,128)(2,1)S(1)} %all_to_all.15.coef_ref), channel_id=1, source_target_pairs={{0,16},{16,0},{1,17},{17,1},{2,18},{18,2},{3,19},{19,3},{4,20},{20... | collective-permute-start | bytes 2457608 | tf_op jit(solution)/shard_map/ppermute | solution.py:332
  79.8 12.5 %own_step.2 = (bf16[40,32,2560]{2,1,0:T(8,128)(2,1)}, bf16[40,16,2560]{2,1,0:T(8,128)(2,1)}, f32[40,2560]{1,0:T(8,128)}) custom-call(s32[1]{0:T(128)S(6)} %sub.16.where, bf16[16,40,640]{2,1,0:T(8,128)(2,1)} %copy-done.9, bf16[40,32,2560]{2,1,0:T(8,128)(2,1)} %bitcast.21, bf16[40,32,2560]{2,1,0:T(8,128)(2,1)} %target_ref.3, ...), custom_call_target="tpu_custom_call" | custom-call | flops 2097152000 | bytes 14000000 | tf_op jit(solution)/shard_map/own_step/pallas_call | solution.py:269
  92.3 0.9 copy-done.10
  93.2 12.6 %own_step.3 = (bf16[40,32,2560]{2,1,0:T(8,128)(2,1)}, bf16[40,16,2560]{2,1,0:T(8,128)(2,1)}, f32[40,2560]{1,0:T(8,128)}) custom-call(s32[1]{0:T(128)} %bitcast.where, bf16[16,40,640]{2,1,0:T(8,128)(2,1)} %copy-done.10, bf16[40,32,2560]{2,1,0:T(8,128)(2,1)} %bitcast.22, bf16[40,32,2560]{2,1,0:T(8,128)(2,1)} %target_ref.3, ...), custom_call_target="tpu_custom_call", output_to_operand_aliasing={{0}: (5, {})} | custom-call | flops 2097152000 | bytes 14000000 | tf_op jit(solution)/shard_map/own_step/pallas_call | solution.py:269
  105.8 11.1 %collective-permute-done.coef_ref = bf16[16,40,640]{2,1,0:T(8,128)(2,1)S(1)} collective-permute-done((bf16[16,40,640]{2,1,0:T(8,128)(2,1)S(1)}, bf16[16,40,640]{2,1,0:T(8,128)(2,1)S(1)}, u32[]{:S(2)}, u32[]{:S(2)}) %collective-permute-start) | collective-permute-done | bytes 819232 | tf_op jit(solution)/shard_map/ppermute | solution.py:332
  116.9 1.9 %copy-done.2 = bf16[40,16,2560]{2,1,0:T(8,128)(2,1)S(1)} copy-done((bf16[40,16,2560]{2,1,0:T(8,128)(2,1)S(1)}, bf16[40,16,2560]{2,1,0:T(8,128)(2,1)}, u32[]{:S(2)}) %copy-start.2) | copy-done | bytes 3276824
  118.9 5.5 %other_step.1 = f32[40,2560]{1,0:T(8,128)S(1)} custom-call(bf16[16,40,640]{2,1,0:T(8,128)(2,1)S(1)} %collective-permute-done.coef_ref, bf16[40,16,2560]{2,1,0:T(8,128)(2,1)} %collective-permute-done.1.state_ref, bf16[40,16,2560]{2,1,0:T(8,128)(2,1)S(1)} %copy-done.2, bf16[640,2560]{1,0:T(8,128)(2,1)S(1)} %copy-done.1), custom_call_target="tpu_custom_call" | custom-call | flops 2097152000 | bytes 12000000 | tf_op jit(solution)/shard_map/other_step/pallas_call | solution.py:312
  124.5 3.3 %collective-permute-start.2 = (bf16[40,2560]{1,0:T(8,128)(2,1)S(1)}, bf16[40,2560]{1,0:T(8,128)(2,1)S(1)}, u32[]{:S(2)}, u32[]{:S(2)}) collective-permute-start(bf16[40,2560]{1,0:T(8,128)(2,1)S(1)} %get-tuple-element.20), channel_id=1, source_target_pairs={{0,16},{16,0},{1,17},{17,1},{2,18},{18,2},{3,19},{19,3},{4,20},{20... | collective-permute-start | bytes 614408 | tf_op jit(solution)/shard_map/ppermute | solution.py:332
  127.8 4.2 %collective-permute-done.2 = bf16[40,2560]{1,0:T(8,128)(2,1)S(1)} collective-permute-done((bf16[40,2560]{1,0:T(8,128)(2,1)S(1)}, bf16[40,2560]{1,0:T(8,128)(2,1)S(1)}, u32[]{:S(2)}, u32[]{:S(2)}) %collective-permute-start.2) | collective-permute-done | bytes 204832 | tf_op jit(solution)/shard_map/ppermute | solution.py:332
  (35 shorter events, 2.4 us)
Async XLA Ops:
  0.6 2.9 %copy-start = (bf16[1,40,32,2560]{3,2,1,0:T(8,128)(2,1)S(1)}, bf16[1,40,32,2560]{3,2,1,0:T(8,128)(2,1)}, u32[]{:S(2)}) copy-start(bf16[1,40,32,2560]{3,2,1,0:T(8,128)(2,1)} %param.10) | copy-start | bytes 19660804
  3.5 1.9 %copy-start.5 = (bf16[2560,640]{1,0:T(8,128)(2,1)S(1)}, bf16[2560,640]{1,0:T(8,128)(2,1)}, u32[]{:S(2)}) copy-start(bf16[2560,640]{1,0:T(8,128)(2,1)} %constant.48.clone.table_ref) | copy-start | bytes 9830404
  13.6 31.9 %all-to-all-start = ((bf16[16,40,1280]{2,1,0:T(8,128)(2,1)}), bf16[16,40,1280]{2,1,0:T(8,128)(2,1)}, u32[]{:S(2)}, u32[]{:S(2)}) async-start(bf16[16,40,1280]{2,1,0:T(8,128)(2,1)} %forward_lon.1), calls=%async_computation | async-start | bytes 3276800 | tf_op jit(solution)/shard_map/all_to_all | solution.py:336
  20.8 7.8 %copy-start.13 = (f32[32,32]{1,0:T(8,128)S(1)}, f32[32,32]{1,0:T(8,128)}, u32[]{:S(2)}) copy-start(f32[32,32]{1,0:T(8,128)} %param.14) | copy-start | bytes 12292
  24.7 92.3 %collective-permute-start.1 = (bf16[40,16,2560]{2,1,0:T(8,128)(2,1)}, bf16[40,16,2560]{2,1,0:T(8,128)(2,1)}, u32[]{:S(2)}, u32[]{:S(2)}) collective-permute-start(bf16[40,16,2560]{2,1,0:T(8,128)(2,1)} %dynamic-slice_bitcast_fusion), channel_id=1, source_target_pairs={{0,16},{16,0},{1,17},{17,1},{2,18},{18,2},{3,19},{19,3},{4,20},{20... | collective-permute-start | bytes 9830408 | tf_op jit(solution)/shard_map/ppermute | solution.py:332
  32.0 4.2 %copy-start.3 = (f32[1,40,32,320]{3,2,1,0:T(8,128)S(1)}, f32[1,40,32,320]{3,2,1,0:T(8,128)}, u32[]{:S(2)}) copy-start(f32[1,40,32,320]{3,2,1,0:T(8,128)} %param.12) | copy-start | bytes 4915204
  32.0 4.2 %copy-start.4 = (f32[40,320]{1,0:T(8,128)S(1)}, f32[40,320]{1,0:T(8,128)}, u32[]{:S(2)}) copy-start(f32[40,320]{1,0:T(8,128)} %gain_ref.1) | copy-start | bytes 153604
  32.0 4.2 %copy-start.6 = (f32[40,1280]{1,0:T(8,128)S(1)}, f32[40,1280]{1,0:T(8,128)}, u32[]{:S(2)}) copy-start(f32[40,1280]{1,0:T(8,128)} %constant.49.clone.pick_ref) | copy-start | bytes 614404
  40.3 1.2 copy-start.7
  41.4 1.2 copy-start.8
  74.0 5.7 %copy-start.9 = (bf16[16,40,640]{2,1,0:T(8,128)(2,1)}, bf16[16,40,640]{2,1,0:T(8,128)(2,1)S(1)}, u32[]{:S(2)}) copy-start(bf16[16,40,640]{2,1,0:T(8,128)(2,1)S(1)} %all_to_all.15.coef_ref) | copy-start | bytes 2457604
  74.0 18.2 %all-to-all-start.1 = ((bf16[16,40,640]{2,1,0:T(8,128)(2,1)}), bf16[16,40,640]{2,1,0:T(8,128)(2,1)S(1)}, u32[]{:S(2)}, u32[]{:S(2)}) async-start(bf16[16,40,640]{2,1,0:T(8,128)(2,1)} %bitcast.26), calls=%async_computation.1 | async-start | bytes 1638400 | tf_op jit(solution)/shard_map/all_to_all | solution.py:336
  77.7 39.3 %collective-permute-start = (bf16[16,40,640]{2,1,0:T(8,128)(2,1)S(1)}, bf16[16,40,640]{2,1,0:T(8,128)(2,1)S(1)}, u32[]{:S(2)}, u32[]{:S(2)}) collective-permute-start(bf16[16,40,640]{2,1,0:T(8,128)(2,1)S(1)} %all_to_all.15.coef_ref), channel_id=1, source_target_pairs={{0,16},{16,0},{1,17},{17,1},{2,18},{18,2},{3,19},{19,3},{4,20},{20... | collective-permute-start | bytes 2457608 | tf_op jit(solution)/shard_map/ppermute | solution.py:332
  92.3 0.9 copy-start.10
  93.2 23.8 %copy-start.1 = (bf16[640,2560]{1,0:T(8,128)(2,1)S(1)}, bf16[640,2560]{1,0:T(8,128)(2,1)}, u32[]{:S(2)}) copy-start(bf16[640,2560]{1,0:T(8,128)(2,1)} %constant.52.clone.table) | copy-start | bytes 9830404
  116.9 1.9 %copy-start.2 = (bf16[40,16,2560]{2,1,0:T(8,128)(2,1)S(1)}, bf16[40,16,2560]{2,1,0:T(8,128)(2,1)}, u32[]{:S(2)}) copy-start(bf16[40,16,2560]{2,1,0:T(8,128)(2,1)} %get-tuple-element.19.own) | copy-start | bytes 9830404
  118.9 5.5 %copy-start.11 = (f32[40,2560]{1,0:T(8,128)S(1)}, f32[40,2560]{1,0:T(8,128)}, u32[]{:S(2)}) copy-start(f32[40,2560]{1,0:T(8,128)} %get-tuple-element.17) | copy-start | bytes 1228804
  118.9 5.5 %copy-start.12 = (f32[40,2560]{1,0:T(8,128)S(1)}, f32[40,2560]{1,0:T(8,128)}, u32[]{:S(2)}) copy-start(f32[40,2560]{1,0:T(8,128)} %get-tuple-element.18) | copy-start | bytes 1228804
  124.5 7.5 %collective-permute-start.2 = (bf16[40,2560]{1,0:T(8,128)(2,1)S(1)}, bf16[40,2560]{1,0:T(8,128)(2,1)S(1)}, u32[]{:S(2)}, u32[]{:S(2)}) collective-permute-start(bf16[40,2560]{1,0:T(8,128)(2,1)S(1)} %get-tuple-element.20), channel_id=1, source_target_pairs={{0,16},{16,0},{1,17},{17,1},{2,18},{18,2},{3,19},{19,3},{4,20},{20... | collective-permute-start | bytes 614408 | tf_op jit(solution)/shard_map/ppermute | solution.py:332

commit v3 on v2

--- a/solution.py
+++ b/solution.py
@@ -234,9 +234,10 @@
 BLOCKS = [range(0, 3), range(3, GROUPS)]
 
 
-def own_kernel(where, coef_ref, state_ref, target_ref, table, *rest):
-    new_ref, new, skill_ref, held, rows_ref, state, target, sems = rest[-8:]
+def own_kernel(where, coef_ref, state_ref, target_ref, table_ref, *rest):
+    new_ref, skill_ref, new, held, rows_ref, state, target, table, sems = rest[-9:]
     levels = pl.ds(pl.multiple_of(HALF * where[0], HALF), HALF)
+    whole = pltpu.make_async_copy(table_ref, table, sems.at[3, 0])
     loads, stores = [], []
     for k, groups in enumerate(BLOCKS):
         rows = slice(8 * groups[0], 8 * groups[-1] + 8)
@@ -249,11 +250,15 @@
         )
         for copy in loads[-1]:
             copy.start()
+        if k == 0:
+            whole.start()
     for k, groups in enumerate(BLOCKS):
         rows = slice(8 * groups[0], 8 * groups[-1] + 8)
         set_rows(coef_ref, held, rows_ref, groups)
         for copy in loads[k]:
             copy.wait()
+        if k == 0:
+            whole.wait()
         for n in range(0, NLON, CHUNK):
             cut = slice(n, n + CHUNK)
             block = rows_ref[HALF * rows.start : HALF * rows.stop]
@@ -268,19 +273,21 @@
 def own_step(where, coef, state, target, table, *into):
     return pl.pallas_call(
         own_kernel,
-        in_specs=[SMEM, VMEM, HBM, HBM, VMEM] + [HBM for _ in into],
-        out_specs=[HBM, VMEM, VMEM],
+        in_specs=[SMEM, VMEM, HBM, HBM, HBM] + [HBM for _ in into],
+        out_specs=[HBM, VMEM, VMEM] if into else [HBM, VMEM],
         out_shape=[
             jax.ShapeDtypeStruct((ROWS, LEVELS, NLON), BF16),
-            jax.ShapeDtypeStruct(FIELD, BF16),
             jax.ShapeDtypeStruct((ROWS, NLON), F32),
-        ],
-        scratch_shapes=[
+        ]
+        + [jax.ShapeDtypeStruct(FIELD, BF16) for _ in into],
+        scratch_shapes=([] if into else [pltpu.VMEM(FIELD, BF16)])
+        + [
             pltpu.VMEM((GROUPS * TILES, 8 * 24, 128), F32),
             pltpu.VMEM((ROWS * HALF, NCOL), BF16),
             pltpu.VMEM(FIELD, BF16),
             pltpu.VMEM(FIELD, BF16),
-            pltpu.SemaphoreType.DMA((3, 2)),
+            pltpu.VMEM((NCOL, NLON), BF16),
+            pltpu.SemaphoreType.DMA((4, 2)),
         ],
         input_output_aliases={5: 0} if into else {},
         cost_estimate=pl.CostEstimate(
@@ -376,8 +383,8 @@
 
     back_table = jnp.asarray(np.ascontiguousarray(table.T))
     mine = member.astype(jnp.int32).reshape(1)
-    new, _, skill_a = own_step(1 - mine, give, field, target, back_table)
-    new, own_half, skill_b = own_step(mine, keep, field, target, back_table, new)
+    new, skill_a = own_step(1 - mine, give, field, target, back_table)
+    new, skill_b, own_half = own_step(mine, keep, field, target, back_table, new)
     part = other_step(partner_coef, partner_state, own_half, back_table)
     rest = to_partner(part.astype(BF16)).astype(F32)
     base = (skill_a + skill_b) * F32(1.0 / LEVELS) - part * F32(0.5 / LEVELS)

time: 133 us -> 133 us (level)
  no operation moved by 1% of the time
where the time goes in v3:
time: 133 us
  Pallas kernels  51.6 us (39%)
  starting transfers between devices  20.1 us (15%)
  blocking collectives  18.7 us (14%)
  local copies, waits for them, and re-layouts  18.6 us (14%)
  waiting for transfers between devices  18.6 us (14%)
  other arithmetic  4.42 us (3%)
    pallas_call x2, Pallas kernels, own_step(): pl.pallas_call(own_kernel, in_specs=[SMEM, VMEM, HBM, HBM, HBM] + [HBM fo...  24 us
    all_to_all x1, blocking collectives, over_lat(): return lax.all_to_all(x, 'lat', split_axis=0, concat_axis=0, tiled=True)  18.7 us
    ppermute x3, waiting for transfers between devices, to_partner(): return lax.ppermute(x, 'member', [(0, 1), (1, 0)])  16.5 us
    all_to_all x2, starting transfers between devices, over_lat(): return lax.all_to_all(x, 'lat', split_axis=0, concat_axis=0, tiled=True)  10.8 us
    unnamed x28, local copies, waits for them, and re-layouts  9.98 us
    pallas_call x1, Pallas kernels, spectral(): pl.pallas_call(spectral_kernel, in_specs=[SMEM, VMEM, HBM, HBM, VMEM, VME...  9.89 us
    ppermute x3, starting transfers between devices, to_partner(): return lax.ppermute(x, 'member', [(0, 1), (1, 0)])  9.28 us
    pallas_call x1, Pallas kernels, forward(): pl.pallas_call(forward_kernel, grid=(GROUPS + 1,), in_specs=[pl.BlockSpec...  8.13 us
  transfers between devices with their start and end apart: 5, of which 3 were waited for; matrix products, arithmetic and copies ran while one was open for 9% of the time, Pallas kernels for 29%

profile of v3, /device:TPU:0, one launch (start us, length us, event | category | flops | bytes accessed | tf_op | source)
XLA Modules:
  0.0 132.8 jit_solution(16135192434399785157)
XLA Ops:
  0.6 2.9 %copy-done = bf16[1,40,32,2560]{3,2,1,0:T(8,128)(2,1)S(1)} copy-done((bf16[1,40,32,2560]{3,2,1,0:T(8,128)(2,1)S(1)}, bf16[1,40,32,2560]{3,2,1,0:T(8,128)(2,1)}, u32[]{:S(2)}) %copy-start) | copy-done | bytes 6553624
  3.5 1.9 %copy-done.5 = bf16[2560,640]{1,0:T(8,128)(2,1)S(1)} copy-done((bf16[2560,640]{1,0:T(8,128)(2,1)S(1)}, bf16[2560,640]{1,0:T(8,128)(2,1)}, u32[]{:S(2)}) %copy-start.5) | copy-done | bytes 3276824
  5.4 8.1 %forward_lon.1 = bf16[16,40,1280]{2,1,0:T(8,128)(2,1)} custom-call(bf16[1280,2560]{1,0:T(8,128)(2,1)S(1)} %bitcast.23, bf16[2560,640]{1,0:T(8,128)(2,1)S(1)} %copy-done.5), custom_call_target="tpu_custom_call" | custom-call | flops 4194304000 | bytes 12000000 | tf_op jit(solution)/shard_map/forward_lon/pallas_call | solution.py:96
  13.6 7.2 %all-to-all-start = ((bf16[16,40,1280]{2,1,0:T(8,128)(2,1)}), bf16[16,40,1280]{2,1,0:T(8,128)(2,1)}, u32[]{:S(2)}, u32[]{:S(2)}) async-start(bf16[16,40,1280]{2,1,0:T(8,128)(2,1)} %forward_lon.1), calls=%async_computation | async-start | bytes 3276800 | tf_op jit(solution)/shard_map/all_to_all | solution.py:343
  20.8 3.9 %dynamic-slice_bitcast_fusion = bf16[40,16,2560]{2,1,0:T(8,128)(2,1)} fusion(bf16[1,40,32,2560]{3,2,1,0:T(8,128)(2,1)} %param.10, s32[]{:T(128)S(6)} %select_n.21), kind=kLoop, calls=%fused_computation | loop fusion | bytes 6553604 | tf_op jit(solution)/shard_map/dynamic_slice | solution.py:351
  24.7 3.9 %collective-permute-start.1 = (bf16[40,16,2560]{2,1,0:T(8,128)(2,1)}, bf16[40,16,2560]{2,1,0:T(8,128)(2,1)}, u32[]{:S(2)}, u32[]{:S(2)}) collective-permute-start(bf16[40,16,2560]{2,1,0:T(8,128)(2,1)} %dynamic-slice_bitcast_fusion), channel_id=1, source_target_pairs={{0,16},{16,0},{1,17},{17,1},{2,18},{18,2},{3,19},{19,3},{4,20},{20... | collective-permute-start | bytes 9830408 | tf_op jit(solution)/shard_map/ppermute | solution.py:339
  29.4 2.6 %broadcast_multiply_fusion = f32[32,8,32,8]{3,2,1,0:T(8,128)} fusion(f32[8,8]{1,0:T(8,128)S(1)} %copy.16, f32[32,32]{1,0:T(8,128)S(1)} %copy.15), kind=kLoop, calls=%fused_computation.1 | loop fusion | flops 65536 | bytes 266496 | tf_op jit(solution)/shard_map/mul | solution.py:359
  32.0 4.2 %mul.43 = f32[256,256]{1,0:T(8,128)S(1)} reshape(f32[32,8,32,8]{3,2,1,0:T(8,128)} %broadcast_multiply_fusion) | data formatting | bytes 524288 | tf_op jit(solution)/shard_map/mul | solution.py:359
  36.2 4.1 %prepare_noise.1 = (f32[320,1280]{1,0:T(8,128)S(1)}, f32[320,1280]{1,0:T(8,128)S(1)}) custom-call(f32[1280,320]{1,0:T(8,128)S(1)} %bitcast.24, f32[256,256]{1,0:T(8,128)S(1)} %copy.17.mix_ref, f32[40,320]{1,0:T(8,128)S(1)} %copy-done.4, f32[40,1280]{1,0:T(8,128)S(1)} %copy-done.6), custom_call_target="tpu_custom_call" | custom-call | flops 1258291200 | bytes 6000000 | tf_op jit(solution)/shard_map/prepare_noise/pallas_call | solution.py:126
  40.3 1.2 copy-done.7
  41.4 1.2 copy-done.8
  43.3 2.1 %all-to-all-done = bf16[16,40,1280]{2,1,0:T(8,128)(2,1)} async-done(((bf16[16,40,1280]{2,1,0:T(8,128)(2,1)}), bf16[16,40,1280]{2,1,0:T(8,128)(2,1)}, u32[]{:S(2)}, u32[]{:S(2)}) %all-to-all-start) | async-done | bytes 1638432 | tf_op jit(solution)/shard_map/all_to_all | solution.py:343
  45.4 9.9 %spectral_step.1 = (bf16[640,640]{1,0:T(8,128)(2,1)}, bf16[640,640]{1,0:T(8,128)(2,1)}) custom-call(s32[1]{0:T(128)} %bitcast.1.odd, bf16[640,1280]{1,0:T(8,128)(2,1)} %bitcast.3.g_ref, bf16[2,640,640]{2,1,0:T(8,128)(2,1)} %constant.50.clone.b_ref, bf16[2,1280,320]{2,1,0:T(8,128)(2,1)} %constant.51.clone.t_ref, bf16[256,256]{1,0:T(8,128)(2,1)} %get-tuple-element.23.mh_ref, ...), custom_call_target="tpu_custom_call" | custom-call | flops 4000000000 | bytes 10000000 | tf_op jit(solution)/shard_map/spectral_step/pallas_call | solution.py:189
  55.3 18.7 %all_to_all.15.coef_ref = bf16[16,40,640]{2,1,0:T(8,128)(2,1)S(1)} all-to-all(bf16[16,40,640]{2,1,0:T(8,128)(2,1)} %bitcast.27), channel_id=1, replica_groups=mesh['ic'=4,'member'=2,'lat'=16] {'lat'}, dimensions={0} | all-to-all | bytes 1638400 | tf_op jit(solution)/shard_map/all_to_all | solution.py:343
  74.0 3.6 %all-to-all-start.1 = ((bf16[16,40,640]{2,1,0:T(8,128)(2,1)}), bf16[16,40,640]{2,1,0:T(8,128)(2,1)S(1)}, u32[]{:S(2)}, u32[]{:S(2)}) async-start(bf16[16,40,640]{2,1,0:T(8,128)(2,1)} %bitcast.26), calls=%async_computation.1 | async-start | bytes 1638400 | tf_op jit(solution)/shard_map/all_to_all | solution.py:343
  77.7 2.1 %collective-permute-start = (bf16[16,40,640]{2,1,0:T(8,128)(2,1)S(1)}, bf16[16,40,640]{2,1,0:T(8,128)(2,1)S(1)}, u32[]{:S(2)}, u32[]{:S(2)}) collective-permute-start(bf16[16,40,640]{2,1,0:T(8,128)(2,1)S(1)} %all_to_all.15.coef_ref), channel_id=1, source_target_pairs={{0,16},{16,0},{1,17},{17,1},{2,18},{18,2},{3,19},{19,3},{4,20},{20... | collective-permute-start | bytes 2457608 | tf_op jit(solution)/shard_map/ppermute | solution.py:339
  79.7 11.4 %own_step.2 = (bf16[40,32,2560]{2,1,0:T(8,128)(2,1)}, f32[40,2560]{1,0:T(8,128)}) custom-call(s32[1]{0:T(128)S(6)} %sub.16.where, bf16[16,40,640]{2,1,0:T(8,128)(2,1)} %copy-done.9, bf16[40,32,2560]{2,1,0:T(8,128)(2,1)} %bitcast.21, bf16[40,32,2560]{2,1,0:T(8,128)(2,1)} %target_ref.3, bf16[640,2560]{1,0:T(8,128)(2,1)} %constant.52.clone.table_ref.table), custom_call_target="tpu_custom_call" | custom-call | flops 2097152000 | bytes 14000000 | tf_op jit(solution)/shard_map/own_step/pallas_call | solution.py:274
  91.1 0.9 copy-done.10
  92.0 12.6 %own_step.3 = (bf16[40,32,2560]{2,1,0:T(8,128)(2,1)}, f32[40,2560]{1,0:T(8,128)}, bf16[40,16,2560]{2,1,0:T(8,128)(2,1)}) custom-call(s32[1]{0:T(128)} %bitcast.where, bf16[16,40,640]{2,1,0:T(8,128)(2,1)} %copy-done.10, bf16[40,32,2560]{2,1,0:T(8,128)(2,1)} %bitcast.22, bf16[40,32,2560]{2,1,0:T(8,128)(2,1)} %target_ref.3, ...), custom_call_target="tpu_custom_call", output_to_operand_aliasing={{0}: (5, {})} | custom-call | flops 2097152000 | bytes 14000000 | tf_op jit(solution)/shard_map/own_step/pallas_call | solution.py:274
  104.7 12.3 %collective-permute-done.coef_ref = bf16[16,40,640]{2,1,0:T(8,128)(2,1)S(1)} collective-permute-done((bf16[16,40,640]{2,1,0:T(8,128)(2,1)S(1)}, bf16[16,40,640]{2,1,0:T(8,128)(2,1)S(1)}, u32[]{:S(2)}, u32[]{:S(2)}) %collective-permute-start) | collective-permute-done | bytes 819232 | tf_op jit(solution)/shard_map/ppermute | solution.py:339
  116.9 1.9 %copy-done.2 = bf16[40,16,2560]{2,1,0:T(8,128)(2,1)S(1)} copy-done((bf16[40,16,2560]{2,1,0:T(8,128)(2,1)S(1)}, bf16[40,16,2560]{2,1,0:T(8,128)(2,1)}, u32[]{:S(2)}) %copy-start.2) | copy-done | bytes 3276824
  118.9 5.5 %other_step.1 = f32[40,2560]{1,0:T(8,128)S(1)} custom-call(bf16[16,40,640]{2,1,0:T(8,128)(2,1)S(1)} %collective-permute-done.coef_ref, bf16[40,16,2560]{2,1,0:T(8,128)(2,1)} %collective-permute-done.1.state_ref, bf16[40,16,2560]{2,1,0:T(8,128)(2,1)S(1)} %copy-done.2, bf16[640,2560]{1,0:T(8,128)(2,1)S(1)} %copy-done.1), custom_call_target="tpu_custom_call" | custom-call | flops 2097152000 | bytes 12000000 | tf_op jit(solution)/shard_map/other_step/pallas_call | solution.py:319
  124.5 3.3 %collective-permute-start.2 = (bf16[40,2560]{1,0:T(8,128)(2,1)S(1)}, bf16[40,2560]{1,0:T(8,128)(2,1)S(1)}, u32[]{:S(2)}, u32[]{:S(2)}) collective-permute-start(bf16[40,2560]{1,0:T(8,128)(2,1)S(1)} %get-tuple-element.20), channel_id=1, source_target_pairs={{0,16},{16,0},{1,17},{17,1},{2,18},{18,2},{3,19},{19,3},{4,20},{20... | collective-permute-start | bytes 614408 | tf_op jit(solution)/shard_map/ppermute | solution.py:339
  127.8 4.2 %collective-permute-done.2 = bf16[40,2560]{1,0:T(8,128)(2,1)S(1)} collective-permute-done((bf16[40,2560]{1,0:T(8,128)(2,1)S(1)}, bf16[40,2560]{1,0:T(8,128)(2,1)S(1)}, u32[]{:S(2)}, u32[]{:S(2)}) %collective-permute-start.2) | collective-permute-done | bytes 204832 | tf_op jit(solution)/shard_map/ppermute | solution.py:339
  (35 shorter events, 2.4 us)
Async XLA Ops:
  0.6 2.9 %copy-start = (bf16[1,40,32,2560]{3,2,1,0:T(8,128)(2,1)S(1)}, bf16[1,40,32,2560]{3,2,1,0:T(8,128)(2,1)}, u32[]{:S(2)}) copy-start(bf16[1,40,32,2560]{3,2,1,0:T(8,128)(2,1)} %param.10) | copy-start | bytes 19660804
  3.5 1.9 %copy-start.5 = (bf16[2560,640]{1,0:T(8,128)(2,1)S(1)}, bf16[2560,640]{1,0:T(8,128)(2,1)}, u32[]{:S(2)}) copy-start(bf16[2560,640]{1,0:T(8,128)(2,1)} %constant.48.clone.table_ref) | copy-start | bytes 9830404
  13.6 31.9 %all-to-all-start = ((bf16[16,40,1280]{2,1,0:T(8,128)(2,1)}), bf16[16,40,1280]{2,1,0:T(8,128)(2,1)}, u32[]{:S(2)}, u32[]{:S(2)}) async-start(bf16[16,40,1280]{2,1,0:T(8,128)(2,1)} %forward_lon.1), calls=%async_computation | async-start | bytes 3276800 | tf_op jit(solution)/shard_map/all_to_all | solution.py:343
  20.8 7.8 %copy-start.13 = (f32[32,32]{1,0:T(8,128)S(1)}, f32[32,32]{1,0:T(8,128)}, u32[]{:S(2)}) copy-start(f32[32,32]{1,0:T(8,128)} %param.14) | copy-start | bytes 12292
  24.7 92.3 %collective-permute-start.1 = (bf16[40,16,2560]{2,1,0:T(8,128)(2,1)}, bf16[40,16,2560]{2,1,0:T(8,128)(2,1)}, u32[]{:S(2)}, u32[]{:S(2)}) collective-permute-start(bf16[40,16,2560]{2,1,0:T(8,128)(2,1)} %dynamic-slice_bitcast_fusion), channel_id=1, source_target_pairs={{0,16},{16,0},{1,17},{17,1},{2,18},{18,2},{3,19},{19,3},{4,20},{20... | collective-permute-start | bytes 9830408 | tf_op jit(solution)/shard_map/ppermute | solution.py:339
  32.0 4.2 %copy-start.3 = (f32[1,40,32,320]{3,2,1,0:T(8,128)S(1)}, f32[1,40,32,320]{3,2,1,0:T(8,128)}, u32[]{:S(2)}) copy-start(f32[1,40,32,320]{3,2,1,0:T(8,128)} %param.12) | copy-start | bytes 4915204
  32.0 4.2 %copy-start.4 = (f32[40,320]{1,0:T(8,128)S(1)}, f32[40,320]{1,0:T(8,128)}, u32[]{:S(2)}) copy-start(f32[40,320]{1,0:T(8,128)} %gain_ref.1) | copy-start | bytes 153604
  32.0 4.2 %copy-start.6 = (f32[40,1280]{1,0:T(8,128)S(1)}, f32[40,1280]{1,0:T(8,128)}, u32[]{:S(2)}) copy-start(f32[40,1280]{1,0:T(8,128)} %constant.49.clone.pick_ref) | copy-start | bytes 614404
  40.3 1.2 copy-start.7
  41.4 1.2 copy-start.8
  74.0 5.7 %copy-start.9 = (bf16[16,40,640]{2,1,0:T(8,128)(2,1)}, bf16[16,40,640]{2,1,0:T(8,128)(2,1)S(1)}, u32[]{:S(2)}) copy-start(bf16[16,40,640]{2,1,0:T(8,128)(2,1)S(1)} %all_to_all.15.coef_ref) | copy-start | bytes 2457604
  74.0 17.1 %all-to-all-start.1 = ((bf16[16,40,640]{2,1,0:T(8,128)(2,1)}), bf16[16,40,640]{2,1,0:T(8,128)(2,1)S(1)}, u32[]{:S(2)}, u32[]{:S(2)}) async-start(bf16[16,40,640]{2,1,0:T(8,128)(2,1)} %bitcast.26), calls=%async_computation.1 | async-start | bytes 1638400 | tf_op jit(solution)/shard_map/all_to_all | solution.py:343
  77.7 39.3 %collective-permute-start = (bf16[16,40,640]{2,1,0:T(8,128)(2,1)S(1)}, bf16[16,40,640]{2,1,0:T(8,128)(2,1)S(1)}, u32[]{:S(2)}, u32[]{:S(2)}) collective-permute-start(bf16[16,40,640]{2,1,0:T(8,128)(2,1)S(1)} %all_to_all.15.coef_ref), channel_id=1, source_target_pairs={{0,16},{16,0},{1,17},{17,1},{2,18},{18,2},{3,19},{19,3},{4,20},{20... | collective-permute-start | bytes 2457608 | tf_op jit(solution)/shard_map/ppermute | solution.py:339
  91.1 0.9 copy-start.10
  92.0 24.9 %copy-start.1 = (bf16[640,2560]{1,0:T(8,128)(2,1)S(1)}, bf16[640,2560]{1,0:T(8,128)(2,1)}, u32[]{:S(2)}) copy-start(bf16[640,2560]{1,0:T(8,128)(2,1)} %constant.52.clone.table_ref.table) | copy-start | bytes 9830404
  116.9 1.9 %copy-start.2 = (bf16[40,16,2560]{2,1,0:T(8,128)(2,1)S(1)}, bf16[40,16,2560]{2,1,0:T(8,128)(2,1)}, u32[]{:S(2)}) copy-start(bf16[40,16,2560]{2,1,0:T(8,128)(2,1)} %get-tuple-element.19.own) | copy-start | bytes 9830404
  118.9 5.5 %copy-start.11 = (f32[40,2560]{1,0:T(8,128)S(1)}, f32[40,2560]{1,0:T(8,128)}, u32[]{:S(2)}) copy-start(f32[40,2560]{1,0:T(8,128)} %get-tuple-element.17) | copy-start | bytes 1228804
  118.9 5.5 %copy-start.12 = (f32[40,2560]{1,0:T(8,128)S(1)}, f32[40,2560]{1,0:T(8,128)}, u32[]{:S(2)}) copy-start(f32[40,2560]{1,0:T(8,128)} %get-tuple-element.18) | copy-start | bytes 1228804
  124.5 7.5 %collective-permute-start.2 = (bf16[40,2560]{1,0:T(8,128)(2,1)S(1)}, bf16[40,2560]{1,0:T(8,128)(2,1)S(1)}, u32[]{:S(2)}, u32[]{:S(2)}) collective-permute-start(bf16[40,2560]{1,0:T(8,128)(2,1)S(1)} %get-tuple-element.20), channel_id=1, source_target_pairs={{0,16},{16,0},{1,17},{17,1},{2,18},{18,2},{3,19},{19,3},{4,20},{20... | collective-permute-start | bytes 614408 | tf_op jit(solution)/shard_map/ppermute | solution.py:339
